TPU v7x, 32 devices: a whole 2x2x4 slice. The times are simulated.
32 devices in a mesh: row: 4 (over x, core), col: 8 (over z, y).
Axes of the slice: x: 2, y: 2, z: 4, core: 2. Of those that a mesh axis runs over, the one named last changes fastest.
Arguments:
- basis_raw: float32 [37, 192, 1024], P(None, 'row', 'col'), may hold values from -4 to 4
- krylov_raw: float32 [4, 37, 34], replicated, may hold values from -6 to 6
- stiffness: float32 [192, 1024], P('row', 'col'), may hold values from -0.4 to 0.4
- rotation: float32 [192, 1024], P('row', 'col'), may hold values from -0.2 to 0.2
Outputs:
- new_columns: float32 [3, 192, 1024], P(None, 'row', 'col')
- coefficients: float32 [4, 40, 37], replicated
- hessenberg: float32 [3, 37], replicated
- gram: float32 [5, 40, 5, 40], replicated
- new_images: float32 [3, 192, 1024], P(None, 'row', 'col')
All inputs are finite; a program needn't handle non-finite values.
Results may differ from a plain program's by a relative error of at most 0.001.
Values sent between devices are 32-bit elements; how exact they have to be, the bound alone decides.
No kernel may reach another device: no remote copies, remote signals or barrier semaphores. Data moves between devices by JAX's collectives and lax.ppermute only.
A program may use at most 64 MiB of HBM per device.

v0:
```python
import jax
import jax.numpy as jnp
from jax import lax
from jax.sharding import PartitionSpec as P

K = 40
STEPS = 3
R = 37
KRYLOV = 34


COUPLING = 0.2
EPSILON = 1e-06
GRAM_SHIFT = 0.05
HIGHEST = lax.Precision.HIGHEST


def padded(x, sides, width):
    for axis, dim in sides:
        peers, length = (lax.axis_size(axis), x.shape[dim])
        up = [(i, (i + 1) % peers) for i in range(peers - 1)]
        down = [(j, i) for i, j in up]
        last = lax.slice_in_dim(x, length - width, length, axis=dim)
        initial = lax.slice_in_dim(x, 0, width, axis=dim)
        before = lax.ppermute(last, axis, up)
        after = lax.ppermute(initial, axis, down)
        x = jnp.concatenate([before, x, after], axis=dim)
    return x


def apply_core(border, diagonal, spin_field):
    middle = border[..., 1:-1, 1:-1]
    left_cells = border[..., 1:-1, :-2]
    right_cells = border[..., 1:-1, 2:]
    upper_cells = border[..., :-2, 1:-1]
    lower_cells = border[..., 2:, 1:-1]
    return (
        diagonal * middle
        - COUPLING * (upper_cells + lower_cells + left_cells + right_cells)
        + spin_field * (right_cells - left_cells)
    )


def lower_inverse(matrix):
    factor = jnp.linalg.cholesky(matrix)
    identity = jnp.eye(matrix.shape[0], dtype=matrix.dtype)
    return lax.linalg.triangular_solve(factor, identity, left_side=True, lower=True)


def trimmed(source, margin):
    if margin == 0:
        return source
    return source[..., margin:-margin, margin:-margin]


def inside_mask(margin, row_count, col_count):
    row_first = lax.axis_index("row") * row_count - margin
    col_first = lax.axis_index("col") * col_count - margin
    row_global = row_first + lax.iota(jnp.int32, row_count + 2 * margin)
    col_global = col_first + lax.iota(jnp.int32, col_count + 2 * margin)
    row_valid = (row_global >= 0) & (row_global < row_count * lax.axis_size("row"))
    col_valid = (col_global >= 0) & (col_global < col_count * lax.axis_size("col"))
    return (row_valid[:, None] & col_valid[None, :]).astype(jnp.float32)


def local(basis_raw, krylov_raw, stiffness, rotation):
    row_count = basis_raw.shape[1]
    col_count = basis_raw.shape[2]
    cell_count = row_count * col_count
    grid_total = cell_count * lax.axis_size("row") * lax.axis_size("col")
    inverse_total = 1.0 / grid_total
    flat_raw = basis_raw.reshape(R, cell_count)
    raw_gram = (
        lax.psum(jnp.dot(flat_raw, flat_raw.T, precision=HIGHEST), ("row", "col")) * inverse_total
    )
    inverse_factor = lower_inverse(raw_gram + GRAM_SHIFT * jnp.eye(R, dtype=jnp.float32))
    prepared = jnp.dot(inverse_factor, flat_raw, precision=HIGHEST)
    basis_rows = jnp.concatenate([prepared, jnp.zeros((STEPS, cell_count), jnp.float32)], 0)
    krylov_flat = krylov_raw.reshape(4 * R, KRYLOV)
    krylov_ortho = jnp.dot(
        krylov_flat,
        lower_inverse(jnp.dot(krylov_flat.T, krylov_flat, precision=HIGHEST)).T,
        precision=HIGHEST,
    )
    krylov_width = KRYLOV + STEPS
    krylov_rows = jnp.pad(krylov_ortho.reshape(4, R, KRYLOV), ((0, 0), (0, STEPS), (0, STEPS)))
    field_rim = padded(jnp.stack([stiffness, rotation]), (("row", 1), ("col", 2)), 3)

    def shrink(extended, margin):
        diagonal = trimmed(field_rim[0], 4 - margin)
        spin_field = trimmed(field_rim[1], 4 - margin)
        return apply_core(extended, diagonal, spin_field) * inside_mask(
            margin - 1, row_count, col_count
        )

    hessen_rows = []
    for turn_index in range(STEPS):
        column = KRYLOV + turn_index
        new_row = R + turn_index
        latest = krylov_rows[:, :, column - 1]
        components = jnp.dot(latest, basis_rows, precision=HIGHEST).reshape(4, row_count, col_count)
        block_rim = padded(components, (("row", 1), ("col", 2)), 4)
        section_four = block_rim[3]
        section_three = trimmed(block_rim[2], 1) + 2.0 * shrink(section_four, 4)
        section_two = (
            trimmed(block_rim[1], 2) + 2.0 * shrink(section_three, 3) - trimmed(section_four, 2)
        )
        section_one = (
            trimmed(block_rim[0], 3) + 2.0 * shrink(section_two, 2) - trimmed(section_three, 2)
        )
        summed = shrink(section_one, 1) - trimmed(section_two, 2)
        target = (0.5 * components[2] - 0.5 * summed).reshape(cell_count)
        first_coef = (
            lax.psum(jnp.dot(basis_rows, target, precision=HIGHEST), ("row", "col")) * inverse_total
        )
        residual_one = target - jnp.dot(first_coef, basis_rows, precision=HIGHEST)
        second_coef = (
            lax.psum(jnp.dot(basis_rows, residual_one, precision=HIGHEST), ("row", "col"))
            * inverse_total
        )
        residual_two = residual_one - jnp.dot(second_coef, basis_rows, precision=HIGHEST)
        square = lax.psum(jnp.sum(residual_two * residual_two), ("row", "col")) * inverse_total
        new_norm = jnp.sqrt(square + EPSILON)
        basis_rows = basis_rows.at[new_row].set(residual_two / new_norm)
        unit_row = (jnp.arange(K) == new_row).astype(jnp.float32)
        expanded = jnp.stack(
            [
                latest[1],
                0.5 * (latest[0] + latest[2]),
                0.5 * (latest[1] + latest[3]),
                first_coef + second_coef + new_norm * unit_row,
            ]
        ).reshape(4 * K)
        matrix_view = krylov_rows.reshape(4 * K, krylov_width)
        first_proj = jnp.dot(expanded, matrix_view, precision=HIGHEST)
        ortho_one = expanded - jnp.dot(matrix_view, first_proj, precision=HIGHEST)
        second_proj = jnp.dot(ortho_one, matrix_view, precision=HIGHEST)
        ortho_two = ortho_one - jnp.dot(matrix_view, second_proj, precision=HIGHEST)
        krylov_norm = jnp.sqrt(jnp.sum(ortho_two * ortho_two) + EPSILON)
        krylov_rows = krylov_rows.at[:, :, column].set((ortho_two / krylov_norm).reshape(4, K))
        unit_column = (jnp.arange(krylov_width) == column).astype(jnp.float32)
        hessen_rows.append(first_proj + second_proj + krylov_norm * unit_column)
    new_columns = basis_rows[R:].reshape(STEPS, row_count, col_count)
    order_zero = padded(basis_rows.reshape(K, row_count, col_count), (("row", 1), ("col", 2)), 4)
    order_one = shrink(order_zero, 4)
    order_two = 2.0 * shrink(order_one, 3) - trimmed(order_zero, 2)
    order_three = 2.0 * shrink(order_two, 2) - trimmed(order_one, 2)
    order_four = 2.0 * shrink(order_three, 1) - trimmed(order_two, 2)
    polynomials = [
        trimmed(order_zero, 4),
        trimmed(order_one, 3),
        trimmed(order_two, 2),
        trimmed(order_three, 1),
        order_four,
    ]
    new_images = polynomials[4][R:]
    band_rows = row_count // 8

    def accumulate(band_index, gram_sum):
        band_start = band_index * band_rows
        band_tile = jnp.concatenate(
            [
                lax.dynamic_slice_in_dim(poly_field, band_start, band_rows, 1).reshape(
                    K, band_rows * col_count
                )
                for poly_field in polynomials
            ],
            0,
        )
        return gram_sum + jnp.dot(band_tile, band_tile.T, precision=HIGHEST)

    local_gram = lax.fori_loop(0, 8, accumulate, jnp.zeros((5 * K, 5 * K), jnp.float32))
    gram = (lax.psum(local_gram, ("row", "col")) * inverse_total).reshape(5, K, 5, K)
    return (new_columns, krylov_rows, jnp.stack(hessen_rows), gram, new_images)


def solution(mesh):
    in_specs = (P(None, "row", "col"), P(), P("row", "col"), P("row", "col"))
    out_specs = (P(None, "row", "col"), P(), P(), P(), P(None, "row", "col"))
    return jax.shard_map(local, mesh=mesh, in_specs=in_specs, out_specs=out_specs, check_vma=False)
```

profile of v0, /device:TPU:0, one launch (start us, length us, event | category | flops | bytes accessed | tf_op | source)
XLA Modules:
  0.0 757.8 jit_solution(2868353420702078962)
XLA Ops:
  24.0 44.1 %psum.77 = f32[37,37]{1,0:T(8,128)S(1)} all-reduce(f32[37,37]{1,0:T(8,128)S(1)} %convolution_bitcast_fusion.2), channel_id=1, replica_groups=mesh['row'=4,'col'=8] {'row','col'}, use_global_device_ids=true, to_apply=%region_0.0 | all-reduce | flops 1369 | bytes 10952 | tf_op jit(solution)/shard_map/psum | solution.py:74
  68.2 3.4 cholesky.31
  82.7 4.2 collective-permute-start.2
  93.3 3.5 collective-permute-start.6
  99.7 4.1 collective-permute-done.7
  107.2 42.9 %psum.78 = f32[40]{0:T(128)S(1)} all-reduce(f32[40]{0:T(128)S(1)} %convolution_bitcast_fusion.8), channel_id=1, replica_groups=mesh['row'=4,'col'=8] {'row','col'}, use_global_device_ids=true, to_apply=%region_5.6 | all-reduce | flops 40 | bytes 320 | tf_op jit(solution)/shard_map/psum | solution.py:114
  151.6 39.8 %psum.79 = f32[40]{0:T(128)S(1)} all-reduce(f32[40]{0:T(128)S(1)} %convolution_bitcast_fusion.7), channel_id=1, replica_groups=mesh['row'=4,'col'=8] {'row','col'}, use_global_device_ids=true, to_apply=%region_6.7 | all-reduce | flops 40 | bytes 320 | tf_op jit(solution)/shard_map/psum | solution.py:118
  192.6 40.4 %psum.80 = f32[]{:T(128)} all-reduce(f32[]{:T(128)} %get-tuple-element.284), channel_id=1, replica_groups=mesh['row'=4,'col'=8] {'row','col'}, use_global_device_ids=true, to_apply=%region_8.9 | all-reduce | flops 1 | bytes 8 | tf_op jit(solution)/shard_map/psum | solution.py:122
  240.4 3.7 collective-permute-done.9
  244.2 3.2 collective-permute-start.10
  256.0 40.2 %psum.81 = f32[40]{0:T(128)S(1)} all-reduce(f32[40]{0:T(128)S(1)} %convolution_bitcast_fusion.6), channel_id=1, replica_groups=mesh['row'=4,'col'=8] {'row','col'}, use_global_device_ids=true, to_apply=%region_10.11 | all-reduce | flops 40 | bytes 320 | tf_op jit(solution)/shard_map/psum | solution.py:114
  297.7 39.7 %psum.82 = f32[40]{0:T(128)S(1)} all-reduce(f32[40]{0:T(128)S(1)} %convolution_bitcast_fusion.5), channel_id=1, replica_groups=mesh['row'=4,'col'=8] {'row','col'}, use_global_device_ids=true, to_apply=%region_11.12 | all-reduce | flops 40 | bytes 320 | tf_op jit(solution)/shard_map/psum | solution.py:118
  338.6 40.4 %psum.83 = f32[]{:T(128)} all-reduce(f32[]{:T(128)} %get-tuple-element.280), channel_id=1, replica_groups=mesh['row'=4,'col'=8] {'row','col'}, use_global_device_ids=true, to_apply=%region_13.14 | all-reduce | flops 1 | bytes 8 | tf_op jit(solution)/shard_map/psum | solution.py:122
  385.8 4.1 collective-permute-done.13
  390.0 3.2 collective-permute-start.14
  395.6 4.4 collective-permute-done.15
  401.8 41.1 %psum.84 = f32[40]{0:T(128)S(1)} all-reduce(f32[40]{0:T(128)S(1)} %convolution_bitcast_fusion.4), channel_id=1, replica_groups=mesh['row'=4,'col'=8] {'row','col'}, use_global_device_ids=true, to_apply=%region_15.16 | all-reduce | flops 40 | bytes 320 | tf_op jit(solution)/shard_map/psum | solution.py:114
  444.4 39.3 %psum.85 = f32[40]{0:T(128)S(1)} all-reduce(f32[40]{0:T(128)S(1)} %convolution_bitcast_fusion.3), channel_id=1, replica_groups=mesh['row'=4,'col'=8] {'row','col'}, use_global_device_ids=true, to_apply=%region_16.17 | all-reduce | flops 40 | bytes 320 | tf_op jit(solution)/shard_map/psum | solution.py:118
  484.9 40.7 %psum.86 = f32[]{:T(128)} all-reduce(f32[]{:T(128)} %get-tuple-element.276), channel_id=1, replica_groups=mesh['row'=4,'col'=8] {'row','col'}, use_global_device_ids=true, to_apply=%region_18.19 | all-reduce | flops 1 | bytes 8 | tf_op jit(solution)/shard_map/psum | solution.py:122
  532.0 3.7 collective-permute-start.16
  538.0 3.2 copy.73
  541.1 3.2 copy.75
  545.7 4.5 collective-permute-start.18
  552.2 4.3 collective-permute-done.19
  558.0 3.4 fusion.5
  563.7 3.1 copy.87
  566.8 5.1 slice_subtract_fusion
  571.9 3.7 slice_subtract_fusion.1
  575.7 5.1 fusion.27
  580.8 3.1 copy.88
  588.9 33.6 %while.20 = (s32[]{:T(128)}, f32[200,200]{1,0:T(8,128)S(1)}, f32[40,48,128]{2,1,0:T(8,128)}, f32[40,48,128]{2,1,0:T(8,128)}, f32[40,48,128]{2,1,0:T(8,128)}, /*i...) while((s32[]{:T(128)}, f32[200,200]{1,0:T(8,128)S(1)}, ...), condition=%wide.region_21.22_spmd.clone, body=%wide.region_20.21_spmd.clone.sunk | while | flops 368720000 | bytes 3556025 | solution.py:172
  624.6 123.8 %all-reduce.4.cloned.1.call-done = f32[200,200]{1,0:T(8,128)} async-done(((f32[200,200]{1,0:T(8,128)}), f32[200,200]{1,0:T(8,128)}) %all-reduce.4.cloned.1.call-update) | async-done | bytes 160016 | tf_op jit(solution)/shard_map/psum | solution.py:173
  (334 shorter events, 128.7 us)
Async XLA Ops:
  7.2 741.3 %all-reduce.4.cloned.1.call-start = ((), (), s32[]{:S(2)}) async-start(), calls=%async_computation | async-start | bytes 409600 | tf_op jit(solution)/shard_map/psum | solution.py:173
  8.0 74.6 %collective-permute-start = (f32[2,3,128]{2,1,0:T(4,128)S(1)}, f32[2,3,128]{2,1,0:T(4,128)S(1)}, u32[]{:S(2)}, u32[]{:S(2)}) collective-permute-start(f32[2,3,128]{2,1,0:T(4,128)S(1)} %get-tuple-element.336), channel_id=1, source_target_pairs={{0,8},{8,16},{16,24},{1,9},{9,17},{17,25},{2,10},{10,18},{18,26},{... | collective-permute-start | bytes 9224 | tf_op jit(solution)/shard_map/ppermute | solution.py:25
  10.3 72.2 %collective-permute-start.1 = (f32[2,3,128]{2,1,0:T(4,128)S(1)}, f32[2,3,128]{2,1,0:T(4,128)S(1)}, u32[]{:S(2)}, u32[]{:S(2)}) collective-permute-start(f32[2,3,128]{2,1,0:T(4,128)S(1)} %get-tuple-element.337), channel_id=1, source_target_pairs={{8,0},{16,8},{24,16},{9,1},{17,9},{25,17},{10,2},{18,10},{26,18},{... | collective-permute-start | bytes 9224 | tf_op jit(solution)/shard_map/ppermute | solution.py:26
  79.4 13.7 %collective-permute-start.4 = (f32[4,4,128]{2,1,0:T(4,128)S(1)}, f32[4,4,128]{2,1,0:T(4,128)S(1)}, u32[]{:S(2)}, u32[]{:S(2)}) collective-permute-start(f32[4,4,128]{2,1,0:T(4,128)S(1)} %get-tuple-element.321), channel_id=1, source_target_pairs={{0,8},{8,16},{16,24},{1,9},{9,17},{17,25},{2,10},{10,18},{18,26},{... | collective-permute-start | bytes 24584 | tf_op jit(solution)/shard_map/ppermute | solution.py:25
  80.7 12.4 %collective-permute-start.5 = (f32[4,4,128]{2,1,0:T(4,128)S(1)}, f32[4,4,128]{2,1,0:T(4,128)S(1)}, u32[]{:S(2)}, u32[]{:S(2)}) collective-permute-start(f32[4,4,128]{2,1,0:T(4,128)S(1)} %get-tuple-element.322), channel_id=1, source_target_pairs={{8,0},{16,8},{24,16},{9,1},{17,9},{25,17},{10,2},{18,10},{26,18},{... | collective-permute-start | bytes 24584 | tf_op jit(solution)/shard_map/ppermute | solution.py:26
  82.1 23.0 %copy-start.15 = (pred[52]{0:T(512)(128)(4,1)}, pred[52]{0:T(512)(128)(4,1)S(1)}, u32[]{:S(2)}) copy-start(pred[52]{0:T(512)(128)(4,1)S(1)} %compare_and_fusion.3) | copy-start | bytes 160
  82.2 22.8 %copy-start.19 = (pred[54]{0:T(512)(128)(4,1)}, pred[54]{0:T(512)(128)(4,1)S(1)}, u32[]{:S(2)}) copy-start(pred[54]{0:T(512)(128)(4,1)S(1)} %compare_and_fusion.1) | copy-start | bytes 166
  82.2 22.9 %copy-start.17 = (pred[132]{0:T(512)(128)(4,1)}, pred[132]{0:T(512)(128)(4,1)S(1)}, u32[]{:S(2)}) copy-start(pred[132]{0:T(512)(128)(4,1)S(1)} %compare_and_fusion.2) | copy-start | bytes 400
  82.2 22.7 %copy-start.21 = (pred[134]{0:T(512)(128)(4,1)}, pred[134]{0:T(512)(128)(4,1)S(1)}, u32[]{:S(2)}) copy-start(pred[134]{0:T(512)(128)(4,1)S(1)} %compare_and_fusion) | copy-start | bytes 406
  82.7 7.3 collective-permute-start.2
  86.9 6.1 collective-permute-start.3
  93.3 5.8 collective-permute-start.6
  96.7 7.1 collective-permute-start.7
  105.4 128.4 %copy-start.23 = (f32[1,40]{1,0:T(1,128)S(1)}, f32[1,40]{1,0:T(1,128)}, u32[]{:S(2)}) copy-start(f32[1,40]{1,0:T(1,128)} %fusion.166) | copy-start | bytes 484
  150.7 100.5 %copy-start.14 = (f32[48,128]{1,0:T(8,128)S(1)}, f32[48,128]{1,0:T(8,128)}, u32[]{:S(2)}) copy-start(f32[48,128]{1,0:T(8,128)} %get-tuple-element.327) | copy-start | bytes 73732
  192.0 62.4 %copy-start.20 = (pred[54]{0:T(512)(128)(4,1)S(1)}, pred[54]{0:T(512)(128)(4,1)}, u32[]{:S(2)}) copy-start(pred[54]{0:T(512)(128)(4,1)} %copy-done.19) | copy-start | bytes 166
  192.0 62.4 %copy-start.22 = (pred[134]{0:T(512)(128)(4,1)S(1)}, pred[134]{0:T(512)(128)(4,1)}, u32[]{:S(2)}) copy-start(pred[134]{0:T(512)(128)(4,1)} %copy-done.21) | copy-start | bytes 406
  192.0 62.6 %copy-start.16 = (pred[52]{0:T(512)(128)(4,1)S(1)}, pred[52]{0:T(512)(128)(4,1)}, u32[]{:S(2)}) copy-start(pred[52]{0:T(512)(128)(4,1)} %copy-done.15) | copy-start | bytes 160
  192.0 62.6 %copy-start.18 = (pred[132]{0:T(512)(128)(4,1)S(1)}, pred[132]{0:T(512)(128)(4,1)}, u32[]{:S(2)}) copy-start(pred[132]{0:T(512)(128)(4,1)} %copy-done.17) | copy-start | bytes 400
  237.2 3.2 collective-permute-start.8
  238.5 5.6 collective-permute-start.9
  244.2 8.5 %collective-permute-start.10 = (f32[4,56,4]{2,1,0:T(8,128)S(1)}, f32[4,56,4]{2,1,0:T(8,128)S(1)}, u32[]{:S(2)}, u32[]{:S(2)}) collective-permute-start(f32[4,56,4]{2,1,0:T(8,128)S(1)} %get-tuple-element.311), channel_id=1, source_target_pairs={{0,1},{1,2},{2,3},{3,4},{4,5},{5,6},{6,7},{8,9},{9,10},{10,11},{11... | collective-permute-start | bytes 10760 | tf_op jit(solution)/shard_map/ppermute | solution.py:25
  247.5 6.8 collective-permute-start.11
  383.0 2.8 collective-permute-start.12
  384.3 5.6 collective-permute-start.13
  390.0 5.6 collective-permute-start.14
  393.3 6.8 collective-permute-start.15
  530.7 10.4 %collective-permute-start.17 = (f32[40,4,128]{2,0,1:T(8,128)}, f32[40,4,128]{2,0,1:T(8,128)}, u32[]{:S(2)}, u32[]{:S(2)}) collective-permute-start(f32[40,4,128]{2,0,1:T(8,128)} %copy.100), channel_id=1, source_target_pairs={{8,0},{16,8},{24,16},{9,1},{17,9},{25,17},{10,2},{18,10},{26,18},{... | collective-permute-start | bytes 245768 | tf_op jit(solution)/shard_map/ppermute | solution.py:26
  532.0 6.0 collective-permute-start.16
  545.7 6.6 collective-permute-start.18
  550.2 6.3 collective-permute-start.19
  588.9 34.3 %copy-start.24 = (f32[1,37]{1,0:T(1,128)S(1)}, f32[1,37]{1,0:T(1,128)}, u32[]{:S(2)}) copy-start(f32[1,37]{1,0:T(1,128)} %fusion.176) | copy-start | bytes 448
  (14 other events, 69.6 us)
Sparse Core Ops, SparseCore 0:
  623.3 125.0 all-reduce.3
where the time goes:
time: 768 us; the launch traced here: 758 us
  blocking collectives  409 us (53%)
  waiting for transfers between devices  151 us (20%)
  local copies, waits for them, and re-layouts  65.8 us (9%)
  other arithmetic  46.6 us (6%)
  starting transfers between devices  41.5 us (5%)
  matrix products  24 us (3%)
  between operations  19.9 us (3%)
    psum x3, blocking collectives, local(): lax.psum(jnp.dot(basis_rows, target, precision=HIGHEST), ('row', 'col'))  124 us
    psum x1, waiting for transfers between devices, local(): lax.psum(local_gram, ('row', 'col')) * inverse_total  124 us
    psum x3, blocking collectives, local(): lax.psum(jnp.sum(residual_two * residual_two), ('row', 'col'))  122 us
    psum x3, blocking collectives, local(): lax.psum(jnp.dot(basis_rows, residual_one, precision=HIGHEST), ('row', 'c...  119 us
    psum x1, blocking collectives, local(): lax.psum(jnp.dot(flat_raw, flat_raw.T, precision=HIGHEST), ('row', 'col'))  44.1 us
    ppermute x10, starting transfers between devices, padded(): before = lax.ppermute(last, axis, up)  28.6 us
    dynamic_slice x24, local copies, waits for them, and re-layouts, accumulate(): lax.dynamic_slice_in_dim(poly_field, band_start, band_rows, 1)  25.9 us
    ppermute x10, waiting for transfers between devices, padded(): after = lax.ppermute(initial, axis, down)  25.1 us
  transfers between devices with their start and end apart: 21, of which 11 were waited for; matrix products, arithmetic and copies ran while one was open for 5% of the time, Pallas kernels for 0%

commit v1 on v0

v1 whole, which is shorter than its diff:
```python
import functools
import jax
import jax.numpy as jnp
from jax import lax
from jax.experimental import pallas as pl
from jax.experimental.pallas import tpu as pltpu
from jax.sharding import PartitionSpec as P

K = 40
STEPS = 3
R = 37
KRYLOV = 34
WIDTH = KRYLOV + STEPS

COUPLING = 0.2
EPSILON = 1e-06
GRAM_SHIFT = 0.05
HIGHEST = lax.Precision.HIGHEST
F32 = jnp.float32
BF16 = jnp.bfloat16

ORDERS = 5
HALO = (ORDERS - 1) * (STEPS + 1)
STRIDE = 48
WIDE = 256
PAD = 128
AXES = ("row", "col")
NT = (((1,), (1,)), ((), ()))


def lower_inverse(matrix):
    factor = jnp.linalg.cholesky(matrix)
    identity = jnp.eye(matrix.shape[0], dtype=matrix.dtype)
    return lax.linalg.triangular_solve(factor, identity, left_side=True, lower=True)


def device_count():
    return lax.axis_size("row") * lax.axis_size("col")


def exchange(spread):
    return lax.all_to_all(spread, AXES, 0, 0, tiled=True)


def shifts(axis):
    peers = lax.axis_size(axis)
    up = [(i, i + 1) for i in range(peers - 1)]
    return up, [(j, i) for i, j in up]


def lanes(shape):
    return lax.broadcasted_iota(jnp.int32, shape, len(shape) - 1)


def sublanes(shape):
    return lax.broadcasted_iota(jnp.int32, shape, len(shape) - 2)


def pack_body(tall_ref, low_ref, high_ref):
    total, slots, cols = tall_ref.shape
    span = cols // HALO
    lane = lanes((slots, cols))

    def group(g, carry):
        low = jnp.zeros((slots, cols), F32)
        high = jnp.zeros((slots, cols), F32)
        for k in range(span):
            cells = tall_ref[g * span + k]
            inside = (lane >= k * HALO) & (lane < (k + 1) * HALO)
            first = pltpu.roll(cells, k * HALO, 1) if k else cells
            turn = (k * HALO + HALO) % cols
            second = pltpu.roll(cells, turn, 1) if turn else cells
            low = jnp.where(inside, first, low)
            high = jnp.where(inside, second, high)
        low_ref[g] = low
        high_ref[g] = high
        return carry

    lax.fori_loop(0, total // span, group, 0)


def sideways(main, side, lane):
    cols = main.shape[-1]
    main_up = pltpu.roll(main, 1, 1)
    side_up = pltpu.roll(side, 1, 1)
    main_down = pltpu.roll(main, cols - 1, 1)
    side_down = pltpu.roll(side, cols - 1, 1)
    first = lane == 0
    last = lane == cols - 1
    left = (jnp.where(first, side_up, main_up), jnp.where(first, main_up, side_up))
    right = (jnp.where(last, side_down, main_down), jnp.where(last, main_down, side_down))
    return left, right


def image_body(
    tall_ref, left_ref, right_ref,
    main_ref, side_ref, coef_ref, hi_ref, lo_ref, gram_ref,
    local_ref, m1, s1, m2, s2, m3, s3, acc_ref,
):
    total, slots, cols = tall_ref.shape
    rows = total - 2 * HALO
    span = cols // HALO
    lane = lanes((slots, cols))
    field = sublanes((slots, cols))

    def unpack(g, carry):
        gathered = [[] for _ in range(8)]
        from_left = left_ref[g]
        from_right = right_ref[g]
        for k in range(span):
            r = g * span + k
            main = tall_ref[r]
            turn = (cols - k * HALO) % cols
            low = pltpu.roll(from_right, turn, 1) if turn else from_right
            turn = (cols - HALO - k * HALO) % cols
            high = pltpu.roll(from_left, turn, 1) if turn else from_left
            side = jnp.where(lane < HALO, low, jnp.where(lane >= cols - HALO, high, 0.0))
            packed = []
            for cells in (main, side):
                spin = cells[R + 1 : R + 2]
                couple = COUPLING * cells[R + 2 : R + 3]
                packed += [cells[R : R + 1], spin - couple, -spin - couple, couple]
            local_ref[r] = jnp.concatenate(packed, 0)
            for q in range(8):
                gathered[q].append(packed[q])
            main_ref[r] = jnp.where(field < R, main, 0.0)
            side_ref[r] = jnp.where(field < R, side, 0.0)
        for q in range(8):
            coef_ref[q, pl.ds(g * span, span), :] = jnp.concatenate(gathered[q], 0)
        return carry

    lax.fori_loop(0, total // span, unpack, 0)

    blank = jnp.zeros((STRIDE - slots, cols), F32)

    def keep(order, r, cells):
        whole = jnp.concatenate([cells, blank], 0)
        high = whole.astype(BF16)
        low = (whole - high.astype(F32)).astype(BF16)
        place = pl.ds(pl.multiple_of((r - HALO) * cols, cols), cols)
        hi_ref[order * STRIDE : (order + 1) * STRIDE, place] = high
        lo_ref[order * STRIDE : (order + 1) * STRIDE, place] = low

    def level(order, source, older, target, need_side):
        source_main, source_side = source

        def one(r, store):
            main = source_main[r]
            side = source_side[r]
            local = local_ref[r]
            left, right = sideways(main, side, lane)
            scale = 1.0 if order == 1 else 2.0
            fresh = scale * (
                local[0:1] * main
                + local[1:2] * right[0]
                + local[2:3] * left[0]
                - local[3:4] * (source_main[r - 1] + source_main[r + 1])
            )
            if older is not None:
                fresh = fresh - older[0][r]
            if target is not None:
                target[0][r] = fresh
            if need_side:
                edge = scale * (
                    local[4:5] * side
                    + local[5:6] * right[1]
                    + local[6:7] * left[1]
                    - local[7:8] * (source_side[r - 1] + source_side[r + 1])
                )
                if older is not None:
                    edge = edge - older[1][r]
                target[1][r] = edge
            if store:
                keep(order, r, fresh)

        reach = ORDERS - 1 - order

        def inner(r, carry):
            one(r, True)
            return carry

        def outer(r, carry):
            one(r, False)
            return carry

        if reach:
            lax.fori_loop(HALO - reach, HALO, outer, 0)
            lax.fori_loop(HALO + rows, HALO + rows + reach, outer, 0)
        lax.fori_loop(HALO, HALO + rows, inner, 0)

    def plain(r, carry):
        keep(0, r, main_ref[r])
        return carry

    lax.fori_loop(HALO, HALO + rows, plain, 0)
    level(1, (main_ref, side_ref), None, (m1, s1), True)
    level(2, (m1, s1), (main_ref, side_ref), (m2, s2), True)
    level(3, (m2, s2), (m1, s1), (m3, s3), True)
    level(4, (m3, s3), (m2, s2), None, False)

    size = ORDERS * STRIDE
    chunk = 4 * cols
    acc_ref[...] = jnp.zeros(acc_ref.shape, F32)

    def product(i, carry):
        place = pl.ds(pl.multiple_of(i * chunk, chunk), chunk)
        high = hi_ref[:, place]
        low = lo_ref[:, place]
        acc_ref[:, :size] += (
            lax.dot_general(high, high, NT, preferred_element_type=F32)
            + lax.dot_general(high, low, NT, preferred_element_type=F32)
            + lax.dot_general(low, high, NT, preferred_element_type=F32)
        )
        return carry

    lax.fori_loop(0, rows * cols // chunk, product, 0)
    lane_wide = lanes((K, WIDE))

    def band(order):
        return acc_ref[order * STRIDE : order * STRIDE + K, :]

    gram_ref[0:K] = band(0)
    gram_ref[K : 2 * K] = jnp.where(
        lane_wide < STRIDE, pltpu.roll(band(4), WIDE - 4 * STRIDE, 1), band(1)
    )
    gram_ref[2 * K : 3 * K] = jnp.where(
        lane_wide < 2 * STRIDE, pltpu.roll(band(3), WIDE - 3 * STRIDE, 1), band(2)
    )
    gram_ref[3 * K :] = jnp.zeros((gram_ref.shape[0] - 3 * K, WIDE), F32)


def absorb(parts, state, turn, inverse_total):
    gram, factor, flipped, square, vectors, pending = state
    new_row = R + turn
    column = KRYLOV + turn
    total = jnp.sum(parts, axis=0, keepdims=True) * inverse_total
    table = jnp.concatenate(
        [total[:, a * WIDE : (a + 1) * WIDE] for a in range(ORDERS)]
        + [jnp.zeros((8 - ORDERS, WIDE), F32)],
        0,
    )
    lane_one = lanes((1, WIDE))
    norm = jnp.sum(jnp.where(lane_one == new_row, table[0:1], 0.0), axis=1, keepdims=True)
    beta = jnp.sqrt(norm + EPSILON)
    sigma = 1.0 / beta
    here = (lanes((K, PAD)) == new_row) & (sublanes((K, PAD)) == new_row)
    factor = jnp.where(here, sigma, factor)
    flipped = jnp.where(here, sigma, flipped)
    square = jnp.where(here, sigma * sigma, square)
    tall = jnp.transpose(
        jnp.concatenate([table[:, :PAD], jnp.zeros((PAD - 8, PAD), F32)], 0)
    )
    lane_gram = lanes((K, WIDE))
    gram = jnp.where(sublanes((K, WIDE)) == new_row, table[0:1], gram)
    for b in range(ORDERS):
        gram = jnp.where(lane_gram == b * STRIDE + new_row, tall[:K, b : b + 1], gram)

    latest = [vectors[j * K : (j + 1) * K, column - 1 : column] for j in range(4)]
    unit = (lax.broadcasted_iota(jnp.int32, (K, 1), 0) == new_row).astype(F32)
    expanded = jnp.concatenate(
        [
            latest[1],
            0.5 * (latest[0] + latest[2]),
            0.5 * (latest[1] + latest[3]),
            pending + beta * unit,
        ],
        0,
    )
    first = jnp.sum(vectors * expanded, axis=0, keepdims=True)
    ortho = expanded - jnp.sum(vectors * first, axis=1, keepdims=True)
    second = jnp.sum(vectors * ortho, axis=0, keepdims=True)
    ortho = ortho - jnp.sum(vectors * second, axis=1, keepdims=True)
    eta = jnp.sqrt(jnp.sum(ortho * ortho, axis=0, keepdims=True) + EPSILON)
    vectors = jnp.where(lanes((4 * K, PAD)) == column, ortho / eta, vectors)
    hessenberg = first + second + eta * (lanes((1, PAD)) == column).astype(F32)
    return (gram, factor, flipped, square, vectors, pending), table, sigma, hessenberg


def coefficients_of(state, turn):
    gram, factor, flipped, square, vectors, _ = state
    column = KRYLOV + turn
    latest = [vectors[j * K : (j + 1) * K, column - 1 : column] for j in range(4)]
    mixes = [jnp.sum(factor * one, axis=0, keepdims=True) for one in latest]
    wide = [jnp.concatenate([m, jnp.zeros((1, WIDE - PAD), F32)], 1) for m in mixes]
    target = 0.5 * wide[2]
    for j in range(4):
        target = target - pltpu.roll(0.5 * wide[j], (j + 1) * STRIDE, 1)
    raw = jnp.sum(gram * target, axis=1, keepdims=True)
    upper = jnp.sum(square * raw, axis=0, keepdims=True)
    inside = jnp.where(lanes((K, PAD)) < K, gram[:, :PAD], 0.0)
    twice = 2.0 * raw - jnp.sum(inside * upper, axis=1, keepdims=True)
    removed = jnp.sum(square * twice, axis=0, keepdims=True)
    pending = jnp.sum(
        jnp.where(lanes((K, PAD)) == sublanes((K, PAD)), jnp.sum(flipped * twice, axis=0, keepdims=True), 0.0),
        axis=1,
        keepdims=True,
    )
    table = jnp.concatenate(mixes + [removed] + [jnp.zeros((PAD - 5, PAD), F32)], 0)
    return jnp.transpose(table), mixes + [removed], pending


def turn_body(turn, inverse_total, count, *refs):
    refs = list(refs)
    parts_ref = refs.pop(0) if turn else None
    state_refs = [refs.pop(0) for _ in range(6)]
    main_ref, side_ref, coef_ref, hi_ref, lo_ref = [refs.pop(0) for _ in range(5)]
    old_fields = [refs.pop(0) for _ in range(turn)]
    old_rows = [refs.pop(0) for _ in range(turn)]
    spread_ref, field_ref, rows_ref, image_ref = [refs.pop(0) for _ in range(4)]
    out_state = [refs.pop(0) for _ in range(6)]
    if turn:
        table_ref, sigma_ref, hessenberg_ref = [refs.pop(0) for _ in range(3)]
    z_ref, t_ref = refs

    state = tuple(r[...] for r in state_refs[:5]) + (state_refs[5][:, 0:1],)
    if turn:
        state, table, sigma, hessenberg = absorb(parts_ref[...], state, turn - 1, inverse_total)
        table_ref[...] = table
        sigma_ref[...] = jnp.broadcast_to(sigma, sigma_ref.shape)
        hessenberg_ref[...] = jnp.broadcast_to(hessenberg, hessenberg_ref.shape)
    upright, mixes, pending = coefficients_of(state, turn)
    for ref, value in zip(out_state[:5], state[:5]):
        ref[...] = value
    out_state[5][...] = jnp.broadcast_to(pending, out_state[5].shape)

    total, slots, cols = main_ref.shape
    rows = total - 2 * HALO
    weights = [jnp.broadcast_to(upright[:K, j : j + 1], (K, cols)) for j in range(5)]

    def mix(g, carry):
        lists = [[[], []] for _ in range(5)]
        for k in range(8):
            for half, ref in enumerate((main_ref, side_ref)):
                cells = ref[g * 8 + k]
                for j in range(5):
                    lists[j][half].append(jnp.sum(weights[j] * cells, axis=0, keepdims=True))
        for j in range(5):
            for half in range(2):
                z_ref[j, half, pl.ds(pl.multiple_of(g * 8, 8), 8), :] = jnp.concatenate(lists[j][half], 0)
        return carry

    lax.fori_loop(0, total // 8, mix, 0)

    z = []
    for j in range(5):
        pair = [z_ref[j, 0], z_ref[j, 1]]
        for s in range(turn):
            scale = mixes[j][:, R + s : R + s + 1]
            pair = [pair[half] + scale * old_fields[s][half] for half in range(2)]
        z.append(pair)

    lane = lanes((total, cols))
    local = [coef_ref[q] for q in range(8)]

    def operate(pair):
        main, side = pair
        left, right = sideways(main, side, lane)
        out = []
        for half, cells in enumerate(pair):
            c = local[4 * half : 4 * half + 4]
            out.append(
                c[0] * cells
                + c[1] * right[half]
                + c[2] * left[half]
                - c[3] * (pltpu.roll(cells, 1, 0) + pltpu.roll(cells, total - 1, 0))
            )
        return out

    def combine(*terms):
        return [sum(w * p[half] for w, p in terms) for half in range(2)]

    four = z[3]
    three = combine((1.0, z[2]), (2.0, operate(four)))
    two = combine((1.0, z[1]), (2.0, operate(three)), (-1.0, four))
    one = combine((1.0, z[0]), (2.0, operate(two)), (-1.0, three))
    summed = combine((1.0, operate(one)), (-1.0, two))
    field = combine((0.5, z[2]), (-0.5, summed), (-1.0, z[4]))
    field_ref[0] = field[0]
    field_ref[1] = field[1]

    images = [field, operate(field)]
    for _ in range(ORDERS - 2):
        images.append(combine((2.0, operate(images[-1])), (-1.0, images[-2])))
    for a in range(ORDERS):
        t_ref[a] = images[a][0]
    image_ref[...] = t_ref[ORDERS - 1, HALO : HALO + rows, :]
    rows_ref[...] = jnp.zeros(rows_ref.shape, F32)
    for r in range(rows):
        for a in range(ORDERS):
            rows_ref[a : a + 1, r * cols : (r + 1) * cols] = t_ref[a, HALO + r : HALO + r + 1, :]

    size = ORDERS * STRIDE
    chunk = 8 * cols
    table = jnp.zeros((8, size), F32)
    own = jnp.zeros((8, 8 * (turn + 1)), F32)
    for i in range(rows * cols // chunk):
        place = slice(i * chunk, (i + 1) * chunk)
        mine = rows_ref[:, place]
        rounded = mine.astype(BF16).astype(F32)
        both = jnp.concatenate([rounded, mine - rounded], 0).astype(BF16)
        by_high = lax.dot_general(both, hi_ref[:, place], NT, preferred_element_type=F32)
        by_low = lax.dot_general(both, lo_ref[:, place], NT, preferred_element_type=F32)
        table = table + (by_high[0:8] + by_high[8:16] + by_low[0:8])
        others = jnp.concatenate([ref[:, place] for ref in old_rows] + [mine], 0)
        own = own + lax.dot_general(mine, others, NT, precision=HIGHEST, preferred_element_type=F32)
    table = jnp.concatenate([table, jnp.zeros((8, WIDE - size), F32)], 1)
    lane_table = lanes((8, WIDE))
    for s in range(turn + 1):
        for b in range(ORDERS):
            table = jnp.where(
                lane_table == b * STRIDE + R + s, own[:, 8 * s + b : 8 * s + b + 1], table
            )
    flat = jnp.concatenate([table[a : a + 1] for a in range(ORDERS)], 1)
    spread_ref[...] = jnp.broadcast_to(flat, (count, ORDERS * WIDE))


def final_body(inverse_total, *refs):
    refs = list(refs)
    parts_ref = refs.pop(0)
    state_refs = [refs.pop(0) for _ in range(6)]
    folded_ref = refs.pop(0)
    old_tables = [refs.pop(0) for _ in range(STEPS - 1)]
    old_sigmas = [refs.pop(0) for _ in range(STEPS - 1)]
    fields = [refs.pop(0) for _ in range(STEPS)]
    images = [refs.pop(0) for _ in range(STEPS)]
    columns_ref, coefficients_ref, hessenberg_ref, gram_ref, image_ref = refs

    state = tuple(r[...] for r in state_refs[:5]) + (state_refs[5][:, 0:1],)
    state, table, sigma, hessenberg = absorb(parts_ref[...], state, STEPS - 1, inverse_total)
    factor = state[1]
    coefficients_ref[...] = state[4]
    hessenberg_ref[...] = jnp.broadcast_to(hessenberg, hessenberg_ref.shape)
    sigmas = [ref[0:1, 0:1] for ref in old_sigmas] + [sigma]
    rows = columns_ref.shape[1]
    for s in range(STEPS):
        columns_ref[s] = sigmas[s] * fields[s][0, HALO : HALO + rows, :]
        image_ref[s] = sigmas[s] * images[s][...]

    lane_wide = lanes((K, WIDE))
    bands = [folded_ref[i * K : (i + 1) * K, :] for i in range(3)]
    upper = [
        bands[0],
        bands[1],
        bands[2],
        pltpu.roll(bands[2], 3 * STRIDE, 1),
        pltpu.roll(bands[1], 4 * STRIDE, 1),
    ]
    blank = jnp.zeros((STRIDE - K, WIDE), F32)
    stacked = []
    for a in range(ORDERS):
        stacked += [jnp.where((lane_wide >= a * STRIDE) & (lane_wide < ORDERS * STRIDE), upper[a], 0.0), blank]
    whole = jnp.concatenate(stacked + [jnp.zeros((WIDE - ORDERS * STRIDE, WIDE), F32)], 0)
    row_id = sublanes((WIDE, WIDE))
    lane_id = lanes((WIDE, WIDE))
    lower = row_id >= (lane_id // STRIDE + 1) * STRIDE
    whole = jnp.where(lower, jnp.transpose(whole), whole)
    for s, one in enumerate([ref[...] for ref in old_tables] + [table]):
        flipped = jnp.transpose(jnp.concatenate([one, jnp.zeros((PAD - 8, WIDE), F32)], 0))
        for a in range(ORDERS):
            whole = jnp.where(row_id == a * STRIDE + R + s, one[a : a + 1, :], whole)
        for a in range(ORDERS):
            whole = jnp.where(lane_id == a * STRIDE + R + s, flipped[:, a : a + 1], whole)
    padded = jnp.concatenate([factor, jnp.zeros((K, WIDE - PAD), F32)], 1)
    padded = jnp.concatenate([padded, blank], 0)
    blocks = [padded] + [pltpu.roll(padded, a * STRIDE, 1) for a in range(1, ORDERS)]
    diagonal = jnp.concatenate(blocks + [jnp.zeros((WIDE - ORDERS * STRIDE, WIDE), F32)], 0)
    half = jnp.dot(diagonal, whole, precision=HIGHEST, preferred_element_type=F32)
    gram_ref[...] = lax.dot_general(half, diagonal, NT, precision=HIGHEST, preferred_element_type=F32)


def shape(*dims, dtype=F32):
    return jax.ShapeDtypeStruct(dims, dtype)


def local(basis_raw, krylov_raw, stiffness, rotation):
    rows = basis_raw.shape[1]
    cols = basis_raw.shape[2]
    cells = rows * cols
    count = device_count()
    inverse_total = 1.0 / (cells * count)
    total = rows + 2 * HALO
    size = ORDERS * STRIDE

    fields = jnp.concatenate(
        [
            jnp.transpose(basis_raw, (1, 0, 2)),
            stiffness[:, None],
            rotation[:, None],
            jnp.ones((rows, 1, cols), F32),
        ],
        1,
    )
    up, down = shifts("row")
    before = lax.ppermute(fields[rows - HALO :], "row", up)
    after = lax.ppermute(fields[:HALO], "row", down)
    tall = jnp.concatenate([before, fields, after], 0)
    strip = shape(total * HALO // cols, K, cols)
    low, high = pl.pallas_call(pack_body, out_shape=(strip, strip), name="pack")(tall)
    up, down = shifts("col")
    from_left = lax.ppermute(high, "col", up)
    from_right = lax.ppermute(low, "col", down)

    level = pltpu.VMEM((total, K, cols), F32)
    main, side, coefs, hi, lo, folded = pl.pallas_call(
        image_body,
        out_shape=(
            shape(total, K, cols),
            shape(total, K, cols),
            shape(8, total, cols),
            shape(size, cells, dtype=BF16),
            shape(size, cells, dtype=BF16),
            shape(PAD, WIDE),
        ),
        scratch_shapes=[pltpu.VMEM((total, 8, cols), F32)]
        + [level] * 6
        + [pltpu.VMEM((size, WIDE), F32)],
        name="images",
    )(tall, from_left, from_right)

    piece = PAD * WIDE // count
    mine = jnp.sum(exchange(folded.reshape(count, piece)), axis=0) * inverse_total
    folded = exchange(jnp.broadcast_to(mine[None], (count, piece))).reshape(PAD, WIDE)

    inverse_factor = lower_inverse(folded[:R, :R] + GRAM_SHIFT * jnp.eye(R, dtype=F32))
    krylov_flat = krylov_raw.reshape(4 * R, KRYLOV)
    krylov_ortho = jnp.dot(
        krylov_flat,
        lower_inverse(jnp.dot(krylov_flat.T, krylov_flat, precision=HIGHEST)).T,
        precision=HIGHEST,
    )
    vectors = jnp.pad(
        krylov_ortho.reshape(4, R, KRYLOV), ((0, 0), (0, K - R), (0, PAD - KRYLOV))
    ).reshape(4 * K, PAD)
    wide = ((0, K - R), (0, PAD - R))
    state = (
        folded[:K],
        jnp.pad(inverse_factor, wide),
        jnp.pad(inverse_factor.T, wide),
        jnp.pad(jnp.dot(inverse_factor.T, inverse_factor, precision=HIGHEST), wide),
        vectors,
        jnp.zeros((K, PAD), F32),
    )
    state_shapes = (
        shape(K, WIDE),
        shape(K, PAD),
        shape(K, PAD),
        shape(K, PAD),
        shape(4 * K, PAD),
        shape(K, PAD),
    )
    parts = ()
    made_fields, made_rows, made_images, tables, sigmas, hessen = [], [], [], [], [], []
    for turn in range(STEPS):
        out_shape = (
            shape(count, ORDERS * WIDE),
            shape(2, total, cols),
            shape(8, cells),
            shape(rows, cols),
        ) + state_shapes
        if turn:
            out_shape += (shape(8, WIDE), shape(8, PAD), shape(8, PAD))
        outs = pl.pallas_call(
            functools.partial(turn_body, turn, inverse_total, count),
            out_shape=out_shape,
            scratch_shapes=[
                pltpu.VMEM((5, 2, total, cols), F32),
                pltpu.VMEM((ORDERS, total, cols), F32),
            ],
            name=f"turn{turn}",
        )(*parts, *state, main, side, coefs, hi, lo, *made_fields, *made_rows)
        made_fields.append(outs[1])
        made_rows.append(outs[2])
        made_images.append(outs[3])
        state = outs[4:10]
        if turn:
            tables.append(outs[10])
            sigmas.append(outs[11])
            hessen.append(outs[12][0, :WIDTH])
        parts = (exchange(outs[0]),)

    new_columns, vectors, last, gram, new_images = pl.pallas_call(
        functools.partial(final_body, inverse_total),
        out_shape=(
            shape(STEPS, rows, cols),
            shape(4 * K, PAD),
            shape(8, PAD),
            shape(WIDE, WIDE),
            shape(STEPS, rows, cols),
        ),
        name="final",
    )(*parts, *state, folded, *tables, *sigmas, *made_fields, *made_images)
    hessen.append(last[0, :WIDTH])
    gram = gram[:size, :size].reshape(ORDERS, STRIDE, ORDERS, STRIDE)[:, :K, :, :K]
    coefficients = vectors.reshape(4, K, PAD)[:, :, :WIDTH]
    return (new_columns, coefficients, jnp.stack(hessen), gram, new_images)


def solution(mesh):
    in_specs = (P(None, "row", "col"), P(), P("row", "col"), P("row", "col"))
    out_specs = (P(None, "row", "col"), P(), P(), P(), P(None, "row", "col"))
    return jax.shard_map(local, mesh=mesh, in_specs=in_specs, out_specs=out_specs, check_vma=False)
```

time: 768 us -> 179 us (0.23); the launches traced: 758 us -> 178 us
  blocking collectives: 409 us -> 20.7 us
  waiting for transfers between devices: 151 us -> 24.4 us
  Pallas kernels: 0 us -> 70.8 us
  local copies, waits for them, and re-layouts: 65.8 us -> 19.9 us
  other arithmetic: 46.6 us -> 17 us
  matrix products: 24 us -> 1.05 us
  between operations: 19.9 us -> 0.95 us
  starting transfers between devices: 41.5 us -> 23.2 us
    psum x10 -> x0, blocking collectives: 409 us -> none  [the longest x3 124 us: local(): lax.psum(jnp.dot(basis_rows, target, precision=HIGHEST), ('row', 'col'))]
    psum x1 -> x0, waiting for transfers between devices: 124 us -> none  [local(): lax.psum(local_gram, ('row', 'col')) * inverse_total]
    pallas_call x0 -> x6, Pallas kernels: none -> 70.8 us  [the longest x1 31.7 us: local(): pl.pallas_call(image_body, out_shape=(shape(total, K, cols), shape(total,...]
    ppermute x20 -> x4, starting transfers between devices: 41.5 us -> 8.42 us  [the longest x1 3.42 us: local(): from_left = lax.ppermute(high, 'col', up)]
    dynamic_slice x24 -> x0, local copies, waits for them, and re-layouts: 25.9 us -> none  [accumulate(): lax.dynamic_slice_in_dim(poly_field, band_start, band_rows, 1)]
    dot_general x37 -> x1, matrix products: 22.2 us -> 0.23 us  [local(): jnp.dot(inverse_factor.T, inverse_factor, precision=HIGHEST)]
    all_to_all x0 -> x2, blocking collectives: none -> 20.7 us  [exchange(): return lax.all_to_all(spread, AXES, 0, 0, tiled=True)]
    ppermute x20 -> x4, waiting for transfers between devices: 26.9 us -> 7.38 us  [the longest x1 3.97 us: local(): after = lax.ppermute(fields[:HALO], 'row', down)]
  transfers between devices with their start and end apart: 21 -> 7, of which waited for: 11 -> 5; matrix products, arithmetic and copies ran while one was open for 5% -> 6% of each run, Pallas kernels for 0% -> 0%
where the time goes in v1:
time: 179 us; the launch traced here: 178 us
  Pallas kernels  70.8 us (40%)
  waiting for transfers between devices  24.4 us (14%)
  starting transfers between devices  23.2 us (13%)
  blocking collectives  20.7 us (12%)
  local copies, waits for them, and re-layouts  19.9 us (11%)
  other arithmetic  17 us (9%)
    pallas_call x1, Pallas kernels, local(): pl.pallas_call(image_body, out_shape=(shape(total, K, cols), shape(total,...  31.7 us
    pallas_call x3, Pallas kernels, local(): pl.pallas_call(functools.partial(turn_body, turn, inverse_total, count),...  30.9 us
    all_to_all x2, blocking collectives, exchange(): return lax.all_to_all(spread, AXES, 0, 0, tiled=True)  20.7 us
    all_to_all x3, waiting for transfers between devices, exchange(): return lax.all_to_all(spread, AXES, 0, 0, tiled=True)  17 us
    all_to_all x3, starting transfers between devices, exchange(): return lax.all_to_all(spread, AXES, 0, 0, tiled=True)  14.8 us
    another operation x6, other arithmetic, lower_inverse(): factor = jnp.linalg.cholesky(matrix)  7.81 us
    another operation x4, other arithmetic, lower_inverse(): lax.linalg.triangular_solve(factor, identity, left_side=True, lower=True)  6.73 us
    unnamed x20, local copies, waits for them, and re-layouts  5.86 us
  transfers between devices with their start and end apart: 7, of which 5 were waited for; matrix products, arithmetic and copies ran while one was open for 6% of the time, Pallas kernels for 0%

profile of v1, /device:TPU:0, one launch (start us, length us, event | category | flops | bytes accessed | tf_op | source)
XLA Modules:
  0.0 178.0 jit_solution(13738102531922862542)
XLA Ops:
  0.7 1.5 copy.50
  2.3 2.4 %collective-permute-start = (f32[16,40,128]{2,1,0:T(8,128)S(1)}, f32[16,40,128]{2,1,0:T(8,128)S(1)}, u32[]{:S(2)}, u32[]{:S(2)}) collective-permute-start(f32[16,40,128]{2,1,0:T(8,128)S(1)} %get-tuple-element.111), channel_id=1, source_target_pairs={{0,8},{8,16},{16,24},{1,9},{9,17},{17,25},{2,10},{10,18},{18,26},{... | collective-permute-start | bytes 983048 | tf_op jit(solution)/shard_map/ppermute | solution.py:494
  4.7 1.3 collective-permute-start.1
  6.4 4.0 %collective-permute-done.1 = f32[16,40,128]{2,1,0:T(8,128)S(1)} collective-permute-done((f32[16,40,128]{2,1,0:T(8,128)S(1)}, f32[16,40,128]{2,1,0:T(8,128)S(1)}, u32[]{:S(2)}, u32[]{:S(2)}) %collective-permute-start.1) | collective-permute-done | bytes 327712 | tf_op jit(solution)/shard_map/ppermute | solution.py:495
  10.3 1.4 pad_maximum_fusion.tall_ref
  11.7 3.6 %pack.1 = (f32[10,40,128]{2,1,0:T(8,128)}, f32[10,40,128]{2,1,0:T(8,128)}) custom-call(f32[80,40,128]{2,1,0:T(8,128)} %pad_maximum_fusion.tall_ref), custom_call_target="tpu_custom_call" | custom-call | tf_op jit(solution)/shard_map/pack/pallas_call | solution.py:498
  15.3 3.4 %collective-permute-start.2 = (f32[10,40,128]{2,1,0:T(8,128)}, f32[10,40,128]{2,1,0:T(8,128)S(1)}, u32[]{:S(2)}, u32[]{:S(2)}) collective-permute-start(f32[10,40,128]{2,1,0:T(8,128)} %get-tuple-element.53), channel_id=1, source_target_pairs={{0,1},{1,2},{2,3},{3,4},{4,5},{5,6},{6,7},{8,9},{9,10},{10,11},{11... | collective-permute-start | bytes 614408 | tf_op jit(solution)/shard_map/ppermute | solution.py:500
  18.7 1.3 collective-permute-start.3
  20.1 3.1 %cholesky.64 = f32[34,34]{1,0:T(8,128)S(1)} custom-call(f32[34,34]{1,0:T(8,128)S(1)} %fusion.5), custom_call_target="Cholesky" | custom-call | tf_op jit(solution)/shard_map/jit(cholesky)/cholesky | solution.py:32
  23.2 3.4 %collective-permute-done.3.right_ref = f32[10,40,128]{2,1,0:T(8,128)S(1)} collective-permute-done((f32[10,40,128]{2,1,0:T(8,128)}, f32[10,40,128]{2,1,0:T(8,128)S(1)}, u32[]{:S(2)}, u32[]{:S(2)}) %collective-permute-start.3) | collective-permute-done | bytes 204832 | tf_op jit(solution)/shard_map/ppermute | solution.py:501
  27.3 31.7 %images.1 = (f32[80,40,128]{2,1,0:T(8,128)}, f32[80,40,128]{2,1,0:T(8,128)}, f32[8,80,128]{2,1,0:T(8,128)}, bf16[240,6144]{1,0:T(8,128)(2,1)}, bf16[240,6144]{1,0:T(8,128)(2,1)}, /*index=5*/f32[128,256]{1,0:T(8,128)}) custom-call(f32[80,40,128]{2,1,0:T(8,128)} %pad_maximum_fusion.tall_ref, f32[10,40,128]{2,1,0:T(8,128)} %copy-done.2, f32[10,40,128]{2,1,0:T(8,128)} %copy-done.3), custom_call_target="tpu_custom_call" | custom-call | tf_op jit(solution)/shard_map/images/pallas_call | solution.py:504
  59.0 1.7 all_to_all.43
  60.7 9.3 %all-to-all-start = ((f32[32,1,1024]{2,1,0:T(1,128)}), f32[32,1,1024]{2,1,0:T(1,128)S(1)}, u32[]{:S(2)}, u32[]{:S(2)}) async-start(f32[32,1,1024]{2,1,0:T(1,128)} %all_to_all.43), calls=%async_computation | async-start | bytes 262144 | tf_op jit(solution)/shard_map/all_to_all | solution.py:42
  71.3 2.6 %custom-call.13 = f32[1,34,34]{1,2,0:T(8,128)S(1)} custom-call(f32[1,34,34]{2,1,0:T(8,128)S(1)} %fusion.2), custom_call_target="InvertDiagBlocksLowerTriangular" | custom-call | tf_op jit(solution)/shard_map/triangular_solve | solution.py:34
  73.9 3.9 %all-to-all-done = f32[32,1,1024]{2,1,0:T(1,128)S(1)} async-done(((f32[32,1,1024]{2,1,0:T(1,128)}), f32[32,1,1024]{2,1,0:T(1,128)S(1)}, u32[]{:S(2)}, u32[]{:S(2)}) %all-to-all-start) | async-done | bytes 131104 | tf_op jit(solution)/shard_map/all_to_all | solution.py:42
  78.6 2.6 %all-to-all-start.1 = ((f32[32,1,1024]{2,1,0:T(1,128)}), f32[32,1,1024]{2,1,0:T(1,128)S(1)}, u32[]{:S(2)}, u32[]{:S(2)}) async-start(f32[32,1,1024]{2,1,0:T(1,128)} %broadcast_in_dim.25), calls=%async_computation.1 | async-start | bytes 262144 | tf_op jit(solution)/shard_map/all_to_all | solution.py:42
  82.6 6.4 %all-to-all-done.1 = f32[32,1,1024]{2,1,0:T(1,128)S(1)} async-done(((f32[32,1,1024]{2,1,0:T(1,128)}), f32[32,1,1024]{2,1,0:T(1,128)S(1)}, u32[]{:S(2)}, u32[]{:S(2)}) %all-to-all-start.1) | async-done | bytes 131104 | tf_op jit(solution)/shard_map/all_to_all | solution.py:42
  89.5 3.4 %cholesky.31 = f32[37,37]{1,0:T(8,128)S(1)} custom-call(f32[37,37]{1,0:T(8,128)S(1)} %fusion.8), custom_call_target="Cholesky" | custom-call | tf_op jit(solution)/shard_map/jit(cholesky)/cholesky | solution.py:32
  94.2 2.8 %custom-call.12 = f32[1,37,37]{1,2,0:T(8,128)S(1)} custom-call(f32[1,37,37]{2,1,0:T(8,128)S(1)} %fusion.1), custom_call_target="InvertDiagBlocksLowerTriangular" | custom-call | tf_op jit(solution)/shard_map/triangular_solve | solution.py:34
  100.8 9.8 %turn0.1 = (f32[32,1280]{1,0:T(8,128)}, f32[2,80,128]{2,1,0:T(8,128)}, f32[8,6144]{1,0:T(8,128)}, f32[48,128]{1,0:T(8,128)}, f32[40,256]{1,0:T(8,128)}, /*index=...) custom-call(f32[40,256]{1,0:T(8,128)} %slice.57.refs_0_, ...), custom_call_target="tpu_custom_call" | custom-call | tf_op jit(solution)/shard_map/turn0/pallas_call | solution.py:562
  110.6 1.1 copy.35
  111.7 10.1 %all_to_all.49 = f32[32,1,1280]{2,1,0:T(1,128)S(1)} all-to-all(f32[32,1,1280]{2,1,0:T(1,128)S(1)} %copy.35), channel_id=1, replica_groups=mesh['row'=4,'col'=8] {'row','col'}, dimensions={0} | all-to-all | bytes 327680 | tf_op jit(solution)/shard_map/all_to_all | solution.py:42
  122.5 10.5 %turn1.1 = (f32[32,1280]{1,0:T(8,128)}, f32[2,80,128]{2,1,0:T(8,128)}, f32[8,6144]{1,0:T(8,128)}, f32[48,128]{1,0:T(8,128)}, f32[40,256]{1,0:T(8,128)}, /*index=...) custom-call(f32[32,1280]{1,0:T(8,128)} %bitcast.55, ...), custom_call_target="tpu_custom_call" | custom-call | tf_op jit(solution)/shard_map/turn1/pallas_call | solution.py:562
  133.0 1.1 copy.36
  134.1 10.7 %all_to_all.50 = f32[32,1,1280]{2,1,0:T(1,128)S(1)} all-to-all(f32[32,1,1280]{2,1,0:T(1,128)S(1)} %copy.36), channel_id=1, replica_groups=mesh['row'=4,'col'=8] {'row','col'}, dimensions={0} | all-to-all | bytes 327680 | tf_op jit(solution)/shard_map/all_to_all | solution.py:42
  145.4 10.6 %turn2.1 = (f32[32,1280]{1,0:T(8,128)}, f32[2,80,128]{2,1,0:T(8,128)}, f32[8,6144]{1,0:T(8,128)}, f32[48,128]{1,0:T(8,128)}, f32[40,256]{1,0:T(8,128)}, /*index=...) custom-call(f32[32,1280]{1,0:T(8,128)} %bitcast.54, ...), custom_call_target="tpu_custom_call" | custom-call | tf_op jit(solution)/shard_map/turn2/pallas_call | solution.py:562
  156.0 1.8 copy.37
  157.8 2.9 %all-to-all-start.4 = ((f32[32,1,1280]{2,1,0:T(1,128)}), f32[32,1,1280]{2,1,0:T(1,128)S(1)}, u32[]{:S(2)}, u32[]{:S(2)}) async-start(f32[32,1,1280]{2,1,0:T(1,128)} %copy.37), calls=%async_computation.4 | async-start | bytes 327680 | tf_op jit(solution)/shard_map/all_to_all | solution.py:42
  162.0 6.6 %all-to-all-done.4 = f32[32,1,1280]{2,1,0:T(1,128)S(1)} async-done(((f32[32,1,1280]{2,1,0:T(1,128)}), f32[32,1,1280]{2,1,0:T(1,128)S(1)}, u32[]{:S(2)}, u32[]{:S(2)}) %all-to-all-start.4) | async-done | bytes 163872 | tf_op jit(solution)/shard_map/all_to_all | solution.py:42
  169.3 4.5 %final.1 = (f32[3,48,128]{2,1,0:T(8,128)}, f32[160,128]{1,0:T(8,128)}, f32[8,128]{1,0:T(8,128)}, f32[256,256]{1,0:T(8,128)}, f32[3,48,128]{2,1,0:T(8,128)}) custom-call(f32[32,1280]{1,0:T(8,128)} %bitcast.53, f32[40,256]{1,0:T(8,128)} %get-tuple-element.80.refs_1_, f32[40,128]{1,0:T(8,128)} %get-tuple-element.81.refs_2_, ...), custom_call_target="tpu_custom_call" | custom-call | tf_op jit(solution)/shard_map/final/pallas_call | solution.py:581
  173.9 1.0 slice.63
  175.1 0.9 copy.39
  (60 shorter events, 15.8 us)
Async XLA Ops:
  0.6 1.6 copy-start.5
  0.6 1.6 copy-start.4
  0.7 5.4 %copy-start.1 = (f32[4,37,34]{1,0,2:T(4,128)S(1)}, f32[4,37,34]{1,0,2:T(4,128)}, u32[]{:S(2)}) copy-start(f32[4,37,34]{1,0,2:T(4,128)} %param.5) | copy-start | bytes 60388
  2.3 4.0 %collective-permute-start = (f32[16,40,128]{2,1,0:T(8,128)S(1)}, f32[16,40,128]{2,1,0:T(8,128)S(1)}, u32[]{:S(2)}, u32[]{:S(2)}) collective-permute-start(f32[16,40,128]{2,1,0:T(8,128)S(1)} %get-tuple-element.111), channel_id=1, source_target_pairs={{0,8},{8,16},{16,24},{1,9},{9,17},{17,25},{2,10},{10,18},{18,26},{... | collective-permute-start | bytes 983048 | tf_op jit(solution)/shard_map/ppermute | solution.py:494
  4.7 5.6 %collective-permute-start.1 = (f32[16,40,128]{2,1,0:T(8,128)S(1)}, f32[16,40,128]{2,1,0:T(8,128)S(1)}, u32[]{:S(2)}, u32[]{:S(2)}) collective-permute-start(f32[16,40,128]{2,1,0:T(8,128)S(1)} %get-tuple-element.112), channel_id=1, source_target_pairs={{8,0},{16,8},{24,16},{9,1},{17,9},{25,17},{10,2},{18,10},{26,18},{... | collective-permute-start | bytes 983048 | tf_op jit(solution)/shard_map/ppermute | solution.py:495
  15.3 7.9 %collective-permute-start.2 = (f32[10,40,128]{2,1,0:T(8,128)}, f32[10,40,128]{2,1,0:T(8,128)S(1)}, u32[]{:S(2)}, u32[]{:S(2)}) collective-permute-start(f32[10,40,128]{2,1,0:T(8,128)} %get-tuple-element.53), channel_id=1, source_target_pairs={{0,1},{1,2},{2,3},{3,4},{4,5},{5,6},{6,7},{8,9},{9,10},{10,11},{11... | collective-permute-start | bytes 614408 | tf_op jit(solution)/shard_map/ppermute | solution.py:500
  18.7 7.9 %collective-permute-start.3 = (f32[10,40,128]{2,1,0:T(8,128)}, f32[10,40,128]{2,1,0:T(8,128)S(1)}, u32[]{:S(2)}, u32[]{:S(2)}) collective-permute-start(f32[10,40,128]{2,1,0:T(8,128)} %get-tuple-element.54), channel_id=1, source_target_pairs={{1,0},{2,1},{3,2},{4,3},{5,4},{6,5},{7,6},{9,8},{10,9},{11,10},{12... | collective-permute-start | bytes 614408 | tf_op jit(solution)/shard_map/ppermute | solution.py:501
  23.2 3.4 %copy-start.2 = (f32[10,40,128]{2,1,0:T(8,128)}, f32[10,40,128]{2,1,0:T(8,128)S(1)}, u32[]{:S(2)}) copy-start(f32[10,40,128]{2,1,0:T(8,128)S(1)} %collective-permute-done.2.left_ref) | copy-start | bytes 614404
  26.6 0.7 copy-start.3
  60.7 17.1 %all-to-all-start = ((f32[32,1,1024]{2,1,0:T(1,128)}), f32[32,1,1024]{2,1,0:T(1,128)S(1)}, u32[]{:S(2)}, u32[]{:S(2)}) async-start(f32[32,1,1024]{2,1,0:T(1,128)} %all_to_all.43), calls=%async_computation | async-start | bytes 262144 | tf_op jit(solution)/shard_map/all_to_all | solution.py:42
  78.6 10.4 %all-to-all-start.1 = ((f32[32,1,1024]{2,1,0:T(1,128)}), f32[32,1,1024]{2,1,0:T(1,128)S(1)}, u32[]{:S(2)}, u32[]{:S(2)}) async-start(f32[32,1,1024]{2,1,0:T(1,128)} %broadcast_in_dim.25), calls=%async_computation.1 | async-start | bytes 262144 | tf_op jit(solution)/shard_map/all_to_all | solution.py:42
  89.4 21.2 %copy-start = (f32[128,256]{1,0:T(8,128)}, f32[128,256]{1,0:T(8,128)S(1)}, u32[]{:S(2)}) copy-start(f32[128,256]{1,0:T(8,128)S(1)} %reshape.68.refs_7_) | copy-start | bytes 393220
  157.8 10.9 %all-to-all-start.4 = ((f32[32,1,1280]{2,1,0:T(1,128)}), f32[32,1,1280]{2,1,0:T(1,128)S(1)}, u32[]{:S(2)}, u32[]{:S(2)}) async-start(f32[32,1,1280]{2,1,0:T(1,128)} %copy.37), calls=%async_computation.4 | async-start | bytes 327680 | tf_op jit(solution)/shard_map/all_to_all | solution.py:42
  175.0 1.6 copy-start.6

commit v2 on v1

--- a/solution.py
+++ b/solution.py
@@ -23,15 +23,12 @@
 HALO = (ORDERS - 1) * (STEPS + 1)
 STRIDE = 48
 WIDE = 256
+UNROLL = 4
+SMALL = pltpu.CompilerParams(vmem_limit_bytes=8 << 20)
+LARGE = pltpu.CompilerParams(vmem_limit_bytes=24 << 20)
 PAD = 128
 AXES = ("row", "col")
 NT = (((1,), (1,)), ((), ()))
-
-
-def lower_inverse(matrix):
-    factor = jnp.linalg.cholesky(matrix)
-    identity = jnp.eye(matrix.shape[0], dtype=matrix.dtype)
-    return lax.linalg.triangular_solve(factor, identity, left_side=True, lower=True)
 
 
 def device_count():
@@ -56,16 +53,17 @@
     return lax.broadcasted_iota(jnp.int32, shape, len(shape) - 2)
 
 
-def pack_body(tall_ref, low_ref, high_ref):
-    total, slots, cols = tall_ref.shape
+def pack_body(before_ref, fields_ref, after_ref, low_ref, high_ref):
+    rows, slots, cols = fields_ref.shape
     span = cols // HALO
     lane = lanes((slots, cols))
-
-    def group(g, carry):
+    edge = HALO // span
+
+    def group(source, shift, g, carry):
         low = jnp.zeros((slots, cols), F32)
         high = jnp.zeros((slots, cols), F32)
         for k in range(span):
-            cells = tall_ref[g * span + k]
+            cells = source[(g - shift) * span + k]
             inside = (lane >= k * HALO) & (lane < (k + 1) * HALO)
             first = pltpu.roll(cells, k * HALO, 1) if k else cells
             turn = (k * HALO + HALO) % cols
@@ -76,7 +74,39 @@
         high_ref[g] = high
         return carry
 
-    lax.fori_loop(0, total // span, group, 0)
+    last = edge + rows // span
+    lax.fori_loop(0, edge, functools.partial(group, before_ref, 0), 0)
+    lax.fori_loop(edge, last, functools.partial(group, fields_ref, edge), 0)
+    lax.fori_loop(last, last + edge, functools.partial(group, after_ref, last), 0)
+
+
+def lower_inverse(matrix, count):
+    lane = lanes(matrix.shape)
+    row = sublanes(matrix.shape)
+    half = PAD // 2
+    work = jnp.where(lane < half, matrix, (lane == row + half).astype(F32))
+    for j in range(count):
+        pivot = work[j : j + 1]
+        ratio = work[:, j : j + 1] / work[j : j + 1, j : j + 1]
+        work = work - jnp.where(row > j, ratio * pivot, 0.0)
+    size = jnp.sum(jnp.where(lane == row, work, 0.0), axis=1, keepdims=True)
+    valid = (row < count) & (lane >= half) & (lane < half + count)
+    size = jnp.where(sublanes(size.shape) < count, size, 1.0)
+    return pltpu.roll(jnp.where(valid, work / jnp.sqrt(size), 0.0), half, 1)
+
+
+def krylov_body(raw_ref, out_ref):
+    groups, length, width = raw_ref.shape
+    out_ref[...] = jnp.zeros(out_ref.shape, F32)
+    for j in range(groups):
+        out_ref[j * K : j * K + length, :width] = raw_ref[j]
+    flat = out_ref[...]
+    square = lax.dot_general(
+        flat, flat, (((0,), (0,)), ((), ())), precision=HIGHEST, preferred_element_type=F32
+    )
+    inverse = lower_inverse(square[:K], width)
+    inverse = jnp.concatenate([inverse, jnp.zeros((PAD - K, PAD), F32)], 0)
+    out_ref[...] = lax.dot_general(flat, inverse, NT, precision=HIGHEST, preferred_element_type=F32)
 
 
 def sideways(main, side, lane):
@@ -93,23 +123,23 @@
 
 
 def image_body(
-    tall_ref, left_ref, right_ref,
-    main_ref, side_ref, coef_ref, hi_ref, lo_ref, gram_ref,
+    before_ref, fields_ref, after_ref, left_ref, right_ref,
+    tall_ref, side_ref, coef_ref, hi_ref, lo_ref, gram_ref,
     local_ref, m1, s1, m2, s2, m3, s3, acc_ref,
 ):
     total, slots, cols = tall_ref.shape
     rows = total - 2 * HALO
     span = cols // HALO
     lane = lanes((slots, cols))
-    field = sublanes((slots, cols))
-
-    def unpack(g, carry):
+
+    def unpack(source, shift, g, carry):
         gathered = [[] for _ in range(8)]
         from_left = left_ref[g]
         from_right = right_ref[g]
         for k in range(span):
             r = g * span + k
-            main = tall_ref[r]
+            main = source[(g - shift) * span + k]
+            tall_ref[r] = main
             turn = (cols - k * HALO) % cols
             low = pltpu.roll(from_right, turn, 1) if turn else from_right
             turn = (cols - HALO - k * HALO) % cols
@@ -120,16 +150,19 @@
                 spin = cells[R + 1 : R + 2]
                 couple = COUPLING * cells[R + 2 : R + 3]
                 packed += [cells[R : R + 1], spin - couple, -spin - couple, couple]
-            local_ref[r] = jnp.concatenate(packed, 0)
+            local_ref[r] = 2.0 * jnp.concatenate(packed, 0)
             for q in range(8):
                 gathered[q].append(packed[q])
-            main_ref[r] = jnp.where(field < R, main, 0.0)
-            side_ref[r] = jnp.where(field < R, side, 0.0)
+            side_ref[r] = side
         for q in range(8):
             coef_ref[q, pl.ds(g * span, span), :] = jnp.concatenate(gathered[q], 0)
         return carry
 
-    lax.fori_loop(0, total // span, unpack, 0)
+    first = HALO // span
+    last = first + rows // span
+    lax.fori_loop(0, first, functools.partial(unpack, before_ref, 0), 0)
+    lax.fori_loop(first, last, functools.partial(unpack, fields_ref, first), 0)
+    lax.fori_loop(last, last + first, functools.partial(unpack, after_ref, last), 0)
 
     blank = jnp.zeros((STRIDE - slots, cols), F32)
 
@@ -149,24 +182,27 @@
             side = source_side[r]
             local = local_ref[r]
             left, right = sideways(main, side, lane)
-            scale = 1.0 if order == 1 else 2.0
-            fresh = scale * (
+            fresh = (
                 local[0:1] * main
                 + local[1:2] * right[0]
                 + local[2:3] * left[0]
                 - local[3:4] * (source_main[r - 1] + source_main[r + 1])
             )
+            if order == 1:
+                fresh = 0.5 * fresh
             if older is not None:
                 fresh = fresh - older[0][r]
             if target is not None:
                 target[0][r] = fresh
             if need_side:
-                edge = scale * (
+                edge = (
                     local[4:5] * side
                     + local[5:6] * right[1]
                     + local[6:7] * left[1]
                     - local[7:8] * (source_side[r - 1] + source_side[r + 1])
                 )
+                if order == 1:
+                    edge = 0.5 * edge
                 if older is not None:
                     edge = edge - older[1][r]
                 target[1][r] = edge
@@ -175,31 +211,29 @@
 
         reach = ORDERS - 1 - order
 
-        def inner(r, carry):
-            one(r, True)
+        def inner(i, carry):
+            for k in range(UNROLL):
+                one(HALO + i * UNROLL + k, True)
             return carry
 
-        def outer(r, carry):
-            one(r, False)
-            return carry
-
-        if reach:
-            lax.fori_loop(HALO - reach, HALO, outer, 0)
-            lax.fori_loop(HALO + rows, HALO + rows + reach, outer, 0)
-        lax.fori_loop(HALO, HALO + rows, inner, 0)
-
-    def plain(r, carry):
-        keep(0, r, main_ref[r])
+        for k in range(reach):
+            one(HALO - 1 - k, False)
+            one(HALO + rows + k, False)
+        lax.fori_loop(0, rows // UNROLL, inner, 0)
+
+    def plain(i, carry):
+        for k in range(UNROLL):
+            keep(0, HALO + i * UNROLL + k, tall_ref[HALO + i * UNROLL + k])
         return carry
 
-    lax.fori_loop(HALO, HALO + rows, plain, 0)
-    level(1, (main_ref, side_ref), None, (m1, s1), True)
-    level(2, (m1, s1), (main_ref, side_ref), (m2, s2), True)
+    lax.fori_loop(0, rows // UNROLL, plain, 0)
+    level(1, (tall_ref, side_ref), None, (m1, s1), True)
+    level(2, (m1, s1), (tall_ref, side_ref), (m2, s2), True)
     level(3, (m2, s2), (m1, s1), (m3, s3), True)
     level(4, (m3, s3), (m2, s2), None, False)
 
     size = ORDERS * STRIDE
-    chunk = 4 * cols
+    chunk = 8 * cols
     acc_ref[...] = jnp.zeros(acc_ref.shape, F32)
 
     def product(i, carry):
@@ -219,21 +253,31 @@
     def band(order):
         return acc_ref[order * STRIDE : order * STRIDE + K, :]
 
-    gram_ref[0:K] = band(0)
-    gram_ref[K : 2 * K] = jnp.where(
-        lane_wide < STRIDE, pltpu.roll(band(4), WIDE - 4 * STRIDE, 1), band(1)
-    )
-    gram_ref[2 * K : 3 * K] = jnp.where(
-        lane_wide < 2 * STRIDE, pltpu.roll(band(3), WIDE - 3 * STRIDE, 1), band(2)
-    )
-    gram_ref[3 * K :] = jnp.zeros((gram_ref.shape[0] - 3 * K, WIDE), F32)
+    bands = [
+        band(0),
+        jnp.where(lane_wide < STRIDE, pltpu.roll(band(4), WIDE - 4 * STRIDE, 1), band(1)),
+        jnp.where(lane_wide < 2 * STRIDE, pltpu.roll(band(3), WIDE - 3 * STRIDE, 1), band(2)),
+    ]
+    for i in range(3):
+        acc_ref[i * K : (i + 1) * K, :] = bands[i]
+    count, _, piece = gram_ref.shape
+    deep = piece // WIDE
+    for i in range(count):
+        for k in range(deep):
+            gram_ref[i, :, k * WIDE : (k + 1) * WIDE] = acc_ref[i * deep + k : i * deep + k + 1, :]
+
+
+def relay_body(parts_ref, spread_ref):
+    total = jnp.sum(parts_ref[...], axis=0)
+    for i in range(spread_ref.shape[0]):
+        spread_ref[i] = total
 
 
 def absorb(parts, state, turn, inverse_total):
     gram, factor, flipped, square, vectors, pending = state
     new_row = R + turn
     column = KRYLOV + turn
-    total = jnp.sum(parts, axis=0, keepdims=True) * inverse_total
+    total = jnp.sum(parts, axis=0) * inverse_total
     table = jnp.concatenate(
         [total[:, a * WIDE : (a + 1) * WIDE] for a in range(ORDERS)]
         + [jnp.zeros((8 - ORDERS, WIDE), F32)],
@@ -301,8 +345,8 @@
 
 def turn_body(turn, inverse_total, count, *refs):
     refs = list(refs)
-    parts_ref = refs.pop(0) if turn else None
-    state_refs = [refs.pop(0) for _ in range(6)]
+    parts_ref = refs.pop(0)
+    state_refs = [refs.pop(0) for _ in range(6 if turn else 1)]
     main_ref, side_ref, coef_ref, hi_ref, lo_ref = [refs.pop(0) for _ in range(5)]
     old_fields = [refs.pop(0) for _ in range(turn)]
     old_rows = [refs.pop(0) for _ in range(turn)]
@@ -310,14 +354,32 @@
     out_state = [refs.pop(0) for _ in range(6)]
     if turn:
         table_ref, sigma_ref, hessenberg_ref = [refs.pop(0) for _ in range(3)]
+    else:
+        folded_ref = refs.pop(0)
     z_ref, t_ref = refs
 
-    state = tuple(r[...] for r in state_refs[:5]) + (state_refs[5][:, 0:1],)
     if turn:
+        state = tuple(r[...] for r in state_refs[:5]) + (state_refs[5][:, 0:1],)
         state, table, sigma, hessenberg = absorb(parts_ref[...], state, turn - 1, inverse_total)
         table_ref[...] = table
         sigma_ref[...] = jnp.broadcast_to(sigma, sigma_ref.shape)
         hessenberg_ref[...] = jnp.broadcast_to(hessenberg, hessenberg_ref.shape)
+    else:
+        pieces, _, piece = parts_ref.shape
+        deep = piece // WIDE
+        for i in range(pieces):
+            for k in range(deep):
+                folded_ref[i * deep + k : i * deep + k + 1, :] = (
+                    parts_ref[i, :, k * WIDE : (k + 1) * WIDE] * inverse_total
+                )
+        gram = folded_ref[0:K, :]
+        diagonal = lanes((K, PAD)) == sublanes((K, PAD))
+        factor = lower_inverse(gram[:, :PAD] + jnp.where(diagonal, GRAM_SHIFT, 0.0), R)
+        square = lax.dot_general(
+            factor, factor, (((0,), (0,)), ((), ())), precision=HIGHEST, preferred_element_type=F32
+        )[:K]
+        flipped = jnp.transpose(jnp.concatenate([factor, jnp.zeros((PAD - K, PAD), F32)], 0))[:K]
+        state = (gram, factor, flipped, square, state_refs[0][...], None)
     upright, mixes, pending = coefficients_of(state, turn)
     for ref, value in zip(out_state[:5], state[:5]):
         ref[...] = value
@@ -325,7 +387,8 @@
 
     total, slots, cols = main_ref.shape
     rows = total - 2 * HALO
-    weights = [jnp.broadcast_to(upright[:K, j : j + 1], (K, cols)) for j in range(5)]
+    raw_only = sublanes((K, cols)) < R
+    weights = [jnp.where(raw_only, upright[:K, j : j + 1], 0.0) for j in range(5)]
 
     def mix(g, carry):
         lists = [[[], []] for _ in range(5)]
@@ -411,7 +474,8 @@
                 lane_table == b * STRIDE + R + s, own[:, 8 * s + b : 8 * s + b + 1], table
             )
     flat = jnp.concatenate([table[a : a + 1] for a in range(ORDERS)], 1)
-    spread_ref[...] = jnp.broadcast_to(flat, (count, ORDERS * WIDE))
+    for i in range(count):
+        spread_ref[i] = flat
 
 
 def final_body(inverse_total, *refs):
@@ -421,6 +485,7 @@
     folded_ref = refs.pop(0)
     old_tables = [refs.pop(0) for _ in range(STEPS - 1)]
     old_sigmas = [refs.pop(0) for _ in range(STEPS - 1)]
+    old_hessen = [refs.pop(0) for _ in range(STEPS - 1)]
     fields = [refs.pop(0) for _ in range(STEPS)]
     images = [refs.pop(0) for _ in range(STEPS)]
     columns_ref, coefficients_ref, hessenberg_ref, gram_ref, image_ref = refs
@@ -428,8 +493,9 @@
     state = tuple(r[...] for r in state_refs[:5]) + (state_refs[5][:, 0:1],)
     state, table, sigma, hessenberg = absorb(parts_ref[...], state, STEPS - 1, inverse_total)
     factor = state[1]
-    coefficients_ref[...] = state[4]
-    hessenberg_ref[...] = jnp.broadcast_to(hessenberg, hessenberg_ref.shape)
+    for j in range(4):
+        coefficients_ref[j] = state[4][j * K : (j + 1) * K, :WIDTH]
+    hessenberg_ref[...] = jnp.concatenate([r[0:1] for r in old_hessen] + [hessenberg], 0)[:, :WIDTH]
     sigmas = [ref[0:1, 0:1] for ref in old_sigmas] + [sigma]
     rows = columns_ref.shape[1]
     for s in range(STEPS):
@@ -493,15 +559,18 @@
     up, down = shifts("row")
     before = lax.ppermute(fields[rows - HALO :], "row", up)
     after = lax.ppermute(fields[:HALO], "row", down)
-    tall = jnp.concatenate([before, fields, after], 0)
+    pieces = (before, fields, after)
     strip = shape(total * HALO // cols, K, cols)
-    low, high = pl.pallas_call(pack_body, out_shape=(strip, strip), name="pack")(tall)
+    low, high = pl.pallas_call(pack_body, out_shape=(strip, strip), name="pack", compiler_params=SMALL)(*pieces)
     up, down = shifts("col")
     from_left = lax.ppermute(high, "col", up)
     from_right = lax.ppermute(low, "col", down)
+    vectors = pl.pallas_call(krylov_body, out_shape=shape(4 * K, PAD), name="krylov", compiler_params=SMALL)(krylov_raw)
+    vectors, from_left = lax.optimization_barrier((vectors, from_left))
 
     level = pltpu.VMEM((total, K, cols), F32)
-    main, side, coefs, hi, lo, folded = pl.pallas_call(
+    piece = PAD * WIDE // count
+    tall, side, coefs, hi, lo, folded = pl.pallas_call(
         image_body,
         out_shape=(
             shape(total, K, cols),
@@ -509,37 +578,19 @@
             shape(8, total, cols),
             shape(size, cells, dtype=BF16),
             shape(size, cells, dtype=BF16),
-            shape(PAD, WIDE),
+            shape(count, 1, piece),
         ),
         scratch_shapes=[pltpu.VMEM((total, 8, cols), F32)]
         + [level] * 6
         + [pltpu.VMEM((size, WIDE), F32)],
-        name="images",
-    )(tall, from_left, from_right)
-
-    piece = PAD * WIDE // count
-    mine = jnp.sum(exchange(folded.reshape(count, piece)), axis=0) * inverse_total
-    folded = exchange(jnp.broadcast_to(mine[None], (count, piece))).reshape(PAD, WIDE)
-
-    inverse_factor = lower_inverse(folded[:R, :R] + GRAM_SHIFT * jnp.eye(R, dtype=F32))
-    krylov_flat = krylov_raw.reshape(4 * R, KRYLOV)
-    krylov_ortho = jnp.dot(
-        krylov_flat,
-        lower_inverse(jnp.dot(krylov_flat.T, krylov_flat, precision=HIGHEST)).T,
-        precision=HIGHEST,
-    )
-    vectors = jnp.pad(
-        krylov_ortho.reshape(4, R, KRYLOV), ((0, 0), (0, K - R), (0, PAD - KRYLOV))
-    ).reshape(4 * K, PAD)
-    wide = ((0, K - R), (0, PAD - R))
-    state = (
-        folded[:K],
-        jnp.pad(inverse_factor, wide),
-        jnp.pad(inverse_factor.T, wide),
-        jnp.pad(jnp.dot(inverse_factor.T, inverse_factor, precision=HIGHEST), wide),
-        vectors,
-        jnp.zeros((K, PAD), F32),
-    )
+        name="images", compiler_params=LARGE,
+    )(*pieces, from_left, from_right)
+
+    mine = pl.pallas_call(
+        relay_body, out_shape=shape(count, 1, piece), name="relay", compiler_params=SMALL
+    )(exchange(folded))
+    parts = exchange(mine)
+
     state_shapes = (
         shape(K, WIDE),
         shape(K, PAD),
@@ -548,17 +599,19 @@
         shape(4 * K, PAD),
         shape(K, PAD),
     )
-    parts = ()
+    state = (vectors,)
     made_fields, made_rows, made_images, tables, sigmas, hessen = [], [], [], [], [], []
     for turn in range(STEPS):
         out_shape = (
-            shape(count, ORDERS * WIDE),
+            shape(count, 1, ORDERS * WIDE),
             shape(2, total, cols),
             shape(8, cells),
             shape(rows, cols),
         ) + state_shapes
         if turn:
             out_shape += (shape(8, WIDE), shape(8, PAD), shape(8, PAD))
+        else:
+            out_shape += (shape(PAD, WIDE),)
         outs = pl.pallas_call(
             functools.partial(turn_body, turn, inverse_total, count),
             out_shape=out_shape,
@@ -566,8 +619,8 @@
                 pltpu.VMEM((5, 2, total, cols), F32),
                 pltpu.VMEM((ORDERS, total, cols), F32),
             ],
-            name=f"turn{turn}",
-        )(*parts, *state, main, side, coefs, hi, lo, *made_fields, *made_rows)
+            name=f"turn{turn}", compiler_params=LARGE,
+        )(parts, *state, tall, side, coefs, hi, lo, *made_fields, *made_rows)
         made_fields.append(outs[1])
         made_rows.append(outs[2])
         made_images.append(outs[3])
@@ -575,24 +628,24 @@
         if turn:
             tables.append(outs[10])
             sigmas.append(outs[11])
-            hessen.append(outs[12][0, :WIDTH])
-        parts = (exchange(outs[0]),)
-
-    new_columns, vectors, last, gram, new_images = pl.pallas_call(
+            hessen.append(outs[12])
+        else:
+            folded = outs[10]
+        parts = exchange(outs[0])
+
+    new_columns, coefficients, hessenberg, gram, new_images = pl.pallas_call(
         functools.partial(final_body, inverse_total),
         out_shape=(
             shape(STEPS, rows, cols),
-            shape(4 * K, PAD),
-            shape(8, PAD),
+            shape(4, K, WIDTH),
+            shape(STEPS, WIDTH),
             shape(WIDE, WIDE),
             shape(STEPS, rows, cols),
         ),
-        name="final",
-    )(*parts, *state, folded, *tables, *sigmas, *made_fields, *made_images)
-    hessen.append(last[0, :WIDTH])
+        name="final", compiler_params=SMALL,
+    )(parts, *state, folded, *tables, *sigmas, *hessen, *made_fields, *made_images)
     gram = gram[:size, :size].reshape(ORDERS, STRIDE, ORDERS, STRIDE)[:, :K, :, :K]
-    coefficients = vectors.reshape(4, K, PAD)[:, :, :WIDTH]
-    return (new_columns, coefficients, jnp.stack(hessen), gram, new_images)
+    return (new_columns, coefficients, hessenberg, gram, new_images)
 
 
 def solution(mesh):

time: 179 us -> 122 us (0.68)
  blocking collectives: 20.7 us -> 59.6 us
  Pallas kernels: 70.8 us -> 42.8 us
  waiting for transfers between devices: 24.4 us -> 3.86 us
  local copies, waits for them, and re-layouts: 19.9 us -> 3.63 us
  other arithmetic: 17 us -> 0.9 us
  starting transfers between devices: 23.2 us -> 10.5 us
    all_to_all x2 -> x5, blocking collectives: 20.7 us -> 59.6 us  [exchange(): return lax.all_to_all(spread, AXES, 0, 0, tiled=True)]
    pallas_call x1, Pallas kernels: 31.7 us -> 13.6 us  [local(): pl.pallas_call(image_body, out_shape=(shape(total, K, cols), shape(total,...]
    all_to_all x3 -> x0, waiting for transfers between devices: 17 us -> none  [exchange(): return lax.all_to_all(spread, AXES, 0, 0, tiled=True)]
    another operation x11 -> x0, other arithmetic: 15.1 us -> none  [the longest x6 7.81 us: lower_inverse(): factor = jnp.linalg.cholesky(matrix)]
    all_to_all x3 -> x0, starting transfers between devices: 14.8 us -> none  [exchange(): return lax.all_to_all(spread, AXES, 0, 0, tiled=True)]
    pallas_call x3, Pallas kernels: 30.9 us -> 21 us  [local(): pl.pallas_call(functools.partial(turn_body, turn, inverse_total, count),...]
    all_to_all x4 -> x0, local copies, waits for them, and re-layouts: 5.6 us -> none  [exchange(): return lax.all_to_all(spread, AXES, 0, 0, tiled=True)]
    ppermute x1, waiting for transfers between devices: 3.97 us -> 0.01 us  [local(): after = lax.ppermute(fields[:HALO], 'row', down)]
  transfers between devices with their start and end apart: 7 -> 4, of which waited for: 5 -> 2; matrix products, arithmetic and copies ran while one was open for 6% -> 0% of each run, Pallas kernels for 0% -> 3%
where the time goes in v2:
time: 122 us
  blocking collectives  59.6 us (49%)
  Pallas kernels  42.8 us (35%)
  starting transfers between devices  10.5 us (9%)
  waiting for transfers between devices  3.86 us (3%)
  local copies, waits for them, and re-layouts  3.63 us (3%)
    all_to_all x5, blocking collectives, exchange(): return lax.all_to_all(spread, AXES, 0, 0, tiled=True)  59.6 us
    pallas_call x3, Pallas kernels, local(): pl.pallas_call(functools.partial(turn_body, turn, inverse_total, count),...  21 us
    pallas_call x1, Pallas kernels, local(): pl.pallas_call(image_body, out_shape=(shape(total, K, cols), shape(total,...  13.6 us
    ppermute x1, starting transfers between devices, local(): from_left = lax.ppermute(high, 'col', up)  4.91 us
    pallas_call x1, Pallas kernels, local(): pl.pallas_call(krylov_body, out_shape=shape(4 * K, PAD), name='krylov', c...  3.56 us
    unnamed x6, local copies, waits for them, and re-layouts  3.22 us
    pallas_call x1, Pallas kernels, local(): pl.pallas_call(functools.partial(final_body, inverse_total), out_shape=(s...  3.16 us
    ppermute x1, starting transfers between devices, local(): before = lax.ppermute(fields[rows - HALO:], 'row', up)  3.05 us
  transfers between devices with their start and end apart: 4, of which 2 were waited for; matrix products, arithmetic and copies ran while one was open for 0% of the time, Pallas kernels for 3%

profile of v2, /device:TPU:0, one launch (start us, length us, event | category | flops | bytes accessed | tf_op | source)
XLA Modules:
  0.0 122.1 jit_solution(15725487346665874452)
XLA Ops:
  0.6 1.5 %copy.18 = f32[37,48,128]{2,0,1:T(8,128)S(1)} copy(f32[37,48,128]{2,1,0:T(8,128)} %param.4) | data formatting | bytes 1818624 | tf_op args[0]
  2.1 0.0 copy-start
  2.1 0.1 pad.3.clone
  2.2 0.9 maximum_maximum_fusion.fields_ref
  3.2 1.3 %collective-permute-start.1 = (f32[16,40,128]{2,1,0:T(8,128)S(1)}, f32[16,40,128]{2,1,0:T(8,128)S(1)}, u32[]{:S(2)}, u32[]{:S(2)}) collective-permute-start(f32[16,40,128]{2,1,0:T(8,128)S(1)} %get-tuple-element.117), channel_id=1, source_target_pairs={{8,0},{16,8},{24,16},{9,1},{17,9},{25,17},{10,2},{18,10},{26,18},{... | collective-permute-start | bytes 983048 | tf_op jit(solution)/shard_map/ppermute | solution.py:561
  4.5 3.1 %collective-permute-start = (f32[16,40,128]{2,1,0:T(8,128)S(1)}, f32[16,40,128]{2,1,0:T(8,128)S(1)}, u32[]{:S(2)}, u32[]{:S(2)}) collective-permute-start(f32[16,40,128]{2,1,0:T(8,128)S(1)} %get-tuple-element.118), channel_id=1, source_target_pairs={{0,8},{8,16},{16,24},{1,9},{9,17},{17,25},{2,10},{10,18},{18,26},{... | collective-permute-start | bytes 983048 | tf_op jit(solution)/shard_map/ppermute | solution.py:560
  7.5 0.0 collective-permute-done.1.after_ref
  7.5 1.2 collective-permute-done.before_ref
  8.7 1.4 %pack.1 = (f32[10,40,128]{2,1,0:T(8,128)S(1)}, f32[10,40,128]{2,1,0:T(8,128)S(1)}) custom-call(f32[16,40,128]{2,1,0:T(8,128)S(1)} %collective-permute-done.before_ref, f32[48,40,128]{2,1,0:T(8,128)S(1)} %maximum_maximum_fusion.fields_ref, f32[16,40,128]{2,1,0:T(8,128)S(1)} %collective-permute-done.1.after_ref), custom_call_target="tpu_custom_call" | custom-call | tf_op jit(solution)/shard_map/pack/pallas_call | solution.py:564
  10.1 4.9 %collective-permute-start.2 = (f32[10,40,128]{2,1,0:T(8,128)S(1)}, f32[10,40,128]{2,1,0:T(8,128)S(1)}, u32[]{:S(2)}, u32[]{:S(2)}) collective-permute-start(f32[10,40,128]{2,1,0:T(8,128)S(1)} %get-tuple-element.56), channel_id=1, source_target_pairs={{0,1},{1,2},{2,3},{3,4},{4,5},{5,6},{6,7},{8,9},{9,10},{10,11},{11... | collective-permute-start | bytes 614408 | tf_op jit(solution)/shard_map/ppermute | solution.py:566
  15.1 1.3 %collective-permute-start.3 = (f32[10,40,128]{2,1,0:T(8,128)S(1)}, f32[10,40,128]{2,1,0:T(8,128)S(1)}, u32[]{:S(2)}, u32[]{:S(2)}) collective-permute-start(f32[10,40,128]{2,1,0:T(8,128)S(1)} %get-tuple-element.58), channel_id=1, source_target_pairs={{1,0},{2,1},{3,2},{4,3},{5,4},{6,5},{7,6},{9,8},{10,9},{11,10},{12... | collective-permute-start | bytes 614408 | tf_op jit(solution)/shard_map/ppermute | solution.py:567
  16.4 0.0 copy-done
  16.4 0.1 copy.14.raw_ref
  16.5 3.6 %krylov.1.refs_1_ = f32[160,128]{1,0:T(8,128)S(1)} custom-call(f32[4,37,34]{2,1,0:T(8,128)S(1)} %copy.14.raw_ref), custom_call_target="tpu_custom_call" | custom-call | tf_op jit(solution)/shard_map/krylov/pallas_call | solution.py:568
  20.1 0.0 collective-permute-done.2.left_ref
  20.1 2.6 %collective-permute-done.3.right_ref = f32[10,40,128]{2,1,0:T(8,128)S(1)} collective-permute-done((f32[10,40,128]{2,1,0:T(8,128)S(1)}, f32[10,40,128]{2,1,0:T(8,128)S(1)}, u32[]{:S(2)}, u32[]{:S(2)}) %collective-permute-start.3) | collective-permute-done | bytes 204832 | tf_op jit(solution)/shard_map/ppermute | solution.py:567
  22.7 13.6 %images.1 = (f32[80,40,128]{2,1,0:T(8,128)S(1)}, f32[80,40,128]{2,1,0:T(8,128)S(1)}, f32[8,80,128]{2,1,0:T(8,128)S(1)}, bf16[240,6144]{1,0:T(8,128)(2,1)S(1)}, b...) custom-call(f32[16,40,128]{2,1,0:T(8,128)S(1)} %collective-permute-done.before_ref, ...), custom_call_target="tpu_custom_call" | custom-call | tf_op jit(solution)/shard_map/images/pallas_call | solution.py:573
  36.3 18.1 %all_to_all.25.parts_ref = f32[32,1,1024]{2,1,0:T(1,128)S(1)} all-to-all(f32[32,1,1024]{2,1,0:T(1,128)S(1)} %get-tuple-element.59), channel_id=1, replica_groups=mesh['row'=4,'col'=8] {'row','col'}, dimensions={0} | all-to-all | bytes 262144 | tf_op jit(solution)/shard_map/all_to_all | solution.py:39
  54.4 0.1 relay.1
  54.5 10.0 %all_to_all.26.refs_0_ = f32[32,1,1024]{2,1,0:T(1,128)S(1)} all-to-all(f32[32,1,1024]{2,1,0:T(1,128)S(1)} %relay.1), channel_id=1, replica_groups=mesh['row'=4,'col'=8] {'row','col'}, dimensions={0} | all-to-all | bytes 262144 | tf_op jit(solution)/shard_map/all_to_all | solution.py:39
  64.4 8.6 %turn0.1 = (f32[32,1,1280]{2,1,0:T(1,128)S(1)}, f32[2,80,128]{2,1,0:T(8,128)S(1)}, f32[8,6144]{1,0:T(8,128)S(1)}, f32[48,128]{1,0:T(8,128)S(1)}, f32[40,256]{1,0...) custom-call(f32[32,1,1024]{2,1,0:T(1,128)S(1)} %all_to_all.26.refs_0, ...), custom_call_target="tpu_custom_call" | custom-call | tf_op jit(solution)/shard_map/turn0/pallas_call | solution.py:615
  73.0 10.2 %all_to_all.27.refs_0_ = f32[32,1,1280]{2,1,0:T(1,128)S(1)} all-to-all(f32[32,1,1280]{2,1,0:T(1,128)S(1)} %get-tuple-element.66), channel_id=1, replica_groups=mesh['row'=4,'col'=8] {'row','col'}, dimensions={0} | all-to-all | bytes 327680 | tf_op jit(solution)/shard_map/all_to_all | solution.py:39
  83.2 6.0 %turn1.1 = (f32[32,1,1280]{2,1,0:T(1,128)S(1)}, f32[2,80,128]{2,1,0:T(8,128)S(1)}, f32[8,6144]{1,0:T(8,128)S(1)}, f32[48,128]{1,0:T(8,128)S(1)}, f32[40,256]{1,0...) custom-call(f32[32,1,1280]{2,1,0:T(1,128)S(1)} %all_to_all.27.refs_0, ...), custom_call_target="tpu_custom_call" | custom-call | tf_op jit(solution)/shard_map/turn1/pallas_call | solution.py:615
  89.2 10.7 %all_to_all.28.refs_0_ = f32[32,1,1280]{2,1,0:T(1,128)S(1)} all-to-all(f32[32,1,1280]{2,1,0:T(1,128)S(1)} %get-tuple-element.75), channel_id=1, replica_groups=mesh['row'=4,'col'=8] {'row','col'}, dimensions={0} | all-to-all | bytes 327680 | tf_op jit(solution)/shard_map/all_to_all | solution.py:39
  99.8 6.5 %turn2.1 = (f32[32,1,1280]{2,1,0:T(1,128)S(1)}, f32[2,80,128]{2,1,0:T(8,128)S(1)}, f32[8,6144]{1,0:T(8,128)}, f32[48,128]{1,0:T(8,128)S(1)}, f32[40,256]{1,0:T(8...) custom-call(f32[32,1,1280]{2,1,0:T(1,128)S(1)} %all_to_all.28.refs_0, ...), custom_call_target="tpu_custom_call" | custom-call | tf_op jit(solution)/shard_map/turn2/pallas_call | solution.py:615
  106.3 10.7 %all_to_all.29.refs_0_ = f32[32,1,1280]{2,1,0:T(1,128)S(1)} all-to-all(f32[32,1,1280]{2,1,0:T(1,128)S(1)} %get-tuple-element.84), channel_id=1, replica_groups=mesh['row'=4,'col'=8] {'row','col'}, dimensions={0} | all-to-all | bytes 327680 | tf_op jit(solution)/shard_map/all_to_all | solution.py:39
  117.0 3.2 %final.1 = (f32[3,48,128]{2,1,0:T(8,128)}, f32[4,40,37]{2,1,0:T(8,128)S(1)}, f32[3,37]{1,0:T(4,128)}, f32[256,256]{1,0:T(8,128)S(1)}, f32[3,48,128]{2,1,0:T(8,128)}) custom-call(f32[32,1,1280]{2,1,0:T(1,128)S(1)} %all_to_all.29.refs_0_, f32[40,256]{1,0:T(8,128)S(1)} %get-tuple-element.85.refs_1_, f32[40,128]{1,0:T(8,128)S(1)} %get-tuple-element.86.refs_2_, ...), custom_call_target="tpu_custom_call" | custom-call | tf_op jit(solution)/shard_map/final/pallas_call | solution.py:636
  120.1 0.7 copy.15
  120.9 0.2 reshape.13
  121.1 0.1 slice.18
  121.2 0.9 copy.16
  (2 shorter events, 0.1 us)
Async XLA Ops:
  2.1 14.3 %copy-start = (f32[4,37,34]{1,0,2:T(4,128)S(1)}, f32[4,37,34]{1,0,2:T(4,128)}, u32[]{:S(2)}) copy-start(f32[4,37,34]{1,0,2:T(4,128)} %param.5) | copy-start | bytes 60388
  3.2 4.4 %collective-permute-start.1 = (f32[16,40,128]{2,1,0:T(8,128)S(1)}, f32[16,40,128]{2,1,0:T(8,128)S(1)}, u32[]{:S(2)}, u32[]{:S(2)}) collective-permute-start(f32[16,40,128]{2,1,0:T(8,128)S(1)} %get-tuple-element.117), channel_id=1, source_target_pairs={{8,0},{16,8},{24,16},{9,1},{17,9},{25,17},{10,2},{18,10},{26,18},{... | collective-permute-start | bytes 983048 | tf_op jit(solution)/shard_map/ppermute | solution.py:561
  4.5 4.3 %collective-permute-start = (f32[16,40,128]{2,1,0:T(8,128)S(1)}, f32[16,40,128]{2,1,0:T(8,128)S(1)}, u32[]{:S(2)}, u32[]{:S(2)}) collective-permute-start(f32[16,40,128]{2,1,0:T(8,128)S(1)} %get-tuple-element.118), channel_id=1, source_target_pairs={{0,8},{8,16},{16,24},{1,9},{9,17},{17,25},{2,10},{10,18},{18,26},{... | collective-permute-start | bytes 983048 | tf_op jit(solution)/shard_map/ppermute | solution.py:560
  10.1 9.9 %collective-permute-start.2 = (f32[10,40,128]{2,1,0:T(8,128)S(1)}, f32[10,40,128]{2,1,0:T(8,128)S(1)}, u32[]{:S(2)}, u32[]{:S(2)}) collective-permute-start(f32[10,40,128]{2,1,0:T(8,128)S(1)} %get-tuple-element.56), channel_id=1, source_target_pairs={{0,1},{1,2},{2,3},{3,4},{4,5},{5,6},{6,7},{8,9},{9,10},{10,11},{11... | collective-permute-start | bytes 614408 | tf_op jit(solution)/shard_map/ppermute | solution.py:566
  15.1 7.7 %collective-permute-start.3 = (f32[10,40,128]{2,1,0:T(8,128)S(1)}, f32[10,40,128]{2,1,0:T(8,128)S(1)}, u32[]{:S(2)}, u32[]{:S(2)}) collective-permute-start(f32[10,40,128]{2,1,0:T(8,128)S(1)} %get-tuple-element.58), channel_id=1, source_target_pairs={{1,0},{2,1},{3,2},{4,3},{5,4},{6,5},{7,6},{9,8},{10,9},{11,10},{12... | collective-permute-start | bytes 614408 | tf_op jit(solution)/shard_map/ppermute | solution.py:567

commit v3 on v2

--- a/solution.py
+++ b/solution.py
@@ -81,18 +81,46 @@
 
 
 def lower_inverse(matrix, count):
-    lane = lanes(matrix.shape)
-    row = sublanes(matrix.shape)
     half = PAD // 2
-    work = jnp.where(lane < half, matrix, (lane == row + half).astype(F32))
-    for j in range(count):
-        pivot = work[j : j + 1]
-        ratio = work[:, j : j + 1] / work[j : j + 1, j : j + 1]
-        work = work - jnp.where(row > j, ratio * pivot, 0.0)
-    size = jnp.sum(jnp.where(lane == row, work, 0.0), axis=1, keepdims=True)
-    valid = (row < count) & (lane >= half) & (lane < half + count)
-    size = jnp.where(sublanes(size.shape) < count, size, 1.0)
-    return pltpu.roll(jnp.where(valid, work / jnp.sqrt(size), 0.0), half, 1)
+    block = 4
+    tile = (8, PAD)
+    groups = range(K // 8)
+    lane = lanes(tile)
+    row = [sublanes(tile) + 8 * g for g in groups]
+    work = []
+    for g in groups:
+        used = (row[g] < count) & (lane < count)
+        left = jnp.where(used, matrix[8 * g : 8 * g + 8], (lane == row[g]).astype(F32))
+        work.append(jnp.where(lane < half, left, (lane == row[g] + half).astype(F32)))
+    for start in range(0, K, block):
+        active = [g for g in groups if 8 * g + 7 > start]
+        spots = range(start, start + block)
+        pivots = [jnp.broadcast_to(work[j // 8][j % 8 : j % 8 + 1], tile) for j in spots]
+        below = [
+            {g: jnp.broadcast_to(work[g][:, j : j + 1], tile) for g in active} for j in spots
+        ]
+        corner = [
+            [jnp.broadcast_to(pivots[i][:, j : j + 1], tile) for j in spots] for i in range(block)
+        ]
+        for i in range(block):
+            inverse = 1.0 / corner[i][i]
+            for k in range(i + 1, block):
+                ratio = corner[i][k] * inverse
+                pivots[k] = pivots[k] - pivots[i] * ratio
+                for g in active:
+                    below[k][g] = below[k][g] - below[i][g] * ratio
+                for other in range(k, block):
+                    corner[k][other] = corner[k][other] - corner[i][other] * ratio
+            below[i] = {g: below[i][g] * inverse for g in active}
+        for g in active:
+            for i in range(block):
+                work[g] = work[g] - jnp.where(row[g] > start + i, below[i][g] * pivots[i], 0.0)
+    out = []
+    for g in groups:
+        size = jnp.sum(jnp.where(lane == row[g], work[g], 0.0), axis=1, keepdims=True)
+        valid = (row[g] < count) & (lane >= half) & (lane < half + count)
+        out.append(pltpu.roll(jnp.where(valid, work[g] / jnp.sqrt(size), 0.0), half, 1))
+    return jnp.concatenate(out, 0)
 
 
 def krylov_body(raw_ref, out_ref):
@@ -124,7 +152,7 @@
 
 def image_body(
     before_ref, fields_ref, after_ref, left_ref, right_ref,
-    tall_ref, side_ref, coef_ref, hi_ref, lo_ref, gram_ref,
+    tall_ref, side_ref, coef_ref, split_ref, gram_ref,
     local_ref, m1, s1, m2, s2, m3, s3, acc_ref,
 ):
     total, slots, cols = tall_ref.shape
@@ -165,14 +193,15 @@
     lax.fori_loop(last, last + first, functools.partial(unpack, after_ref, last), 0)
 
     blank = jnp.zeros((STRIDE - slots, cols), F32)
+    size = ORDERS * STRIDE
 
     def keep(order, r, cells):
         whole = jnp.concatenate([cells, blank], 0)
         high = whole.astype(BF16)
         low = (whole - high.astype(F32)).astype(BF16)
         place = pl.ds(pl.multiple_of((r - HALO) * cols, cols), cols)
-        hi_ref[order * STRIDE : (order + 1) * STRIDE, place] = high
-        lo_ref[order * STRIDE : (order + 1) * STRIDE, place] = low
+        split_ref[order * STRIDE : (order + 1) * STRIDE, place] = high
+        split_ref[size + order * STRIDE : size + (order + 1) * STRIDE, place] = low
 
     def level(order, source, older, target, need_side):
         source_main, source_side = source
@@ -232,22 +261,21 @@
     level(3, (m2, s2), (m1, s1), (m3, s3), True)
     level(4, (m3, s3), (m2, s2), None, False)
 
-    size = ORDERS * STRIDE
-    chunk = 8 * cols
-    acc_ref[...] = jnp.zeros(acc_ref.shape, F32)
-
-    def product(i, carry):
-        place = pl.ds(pl.multiple_of(i * chunk, chunk), chunk)
-        high = hi_ref[:, place]
-        low = lo_ref[:, place]
-        acc_ref[:, :size] += (
-            lax.dot_general(high, high, NT, preferred_element_type=F32)
-            + lax.dot_general(high, low, NT, preferred_element_type=F32)
-            + lax.dot_general(low, high, NT, preferred_element_type=F32)
+    chunk = rows * cols // 3
+    for i in range(3):
+        place = slice(i * chunk, (i + 1) * chunk)
+        part = lax.dot_general(
+            split_ref[:, place], split_ref[:size, place], NT, preferred_element_type=F32
         )
-        return carry
-
-    lax.fori_loop(0, rows * cols // chunk, product, 0)
+        if i:
+            acc_ref[:, :size] += part
+        else:
+            acc_ref[:, :size] = part
+    cross = jnp.concatenate(
+        [acc_ref[size:, :size], jnp.zeros((size, WIDE - size), F32)], 1
+    )
+    cross = jnp.concatenate([cross, jnp.zeros((WIDE - size, WIDE), F32)], 0)
+    acc_ref[:size, :size] += (cross + jnp.transpose(cross))[:size, :size]
     lane_wide = lanes((K, WIDE))
 
     def band(order):
@@ -347,7 +375,7 @@
     refs = list(refs)
     parts_ref = refs.pop(0)
     state_refs = [refs.pop(0) for _ in range(6 if turn else 1)]
-    main_ref, side_ref, coef_ref, hi_ref, lo_ref = [refs.pop(0) for _ in range(5)]
+    main_ref, side_ref, coef_ref, split_ref = [refs.pop(0) for _ in range(4)]
     old_fields = [refs.pop(0) for _ in range(turn)]
     old_rows = [refs.pop(0) for _ in range(turn)]
     spread_ref, field_ref, rows_ref, image_ref = [refs.pop(0) for _ in range(4)]
@@ -356,7 +384,7 @@
         table_ref, sigma_ref, hessenberg_ref = [refs.pop(0) for _ in range(3)]
     else:
         folded_ref = refs.pop(0)
-    z_ref, t_ref = refs
+    z_ref, t_ref, flat_ref = refs
 
     if turn:
         state = tuple(r[...] for r in state_refs[:5]) + (state_refs[5][:, 0:1],)
@@ -447,31 +475,39 @@
     for a in range(ORDERS):
         t_ref[a] = images[a][0]
     image_ref[...] = t_ref[ORDERS - 1, HALO : HALO + rows, :]
-    rows_ref[...] = jnp.zeros(rows_ref.shape, F32)
+    t_ref[ORDERS:] = jnp.zeros((8 - ORDERS, total, cols), F32)
     for r in range(rows):
-        for a in range(ORDERS):
-            rows_ref[a : a + 1, r * cols : (r + 1) * cols] = t_ref[a, HALO + r : HALO + r + 1, :]
+        flat_ref[:, r * cols : (r + 1) * cols] = t_ref[:, HALO + r, :]
 
     size = ORDERS * STRIDE
-    chunk = 8 * cols
-    table = jnp.zeros((8, size), F32)
-    own = jnp.zeros((8, 8 * (turn + 1)), F32)
-    for i in range(rows * cols // chunk):
+    chunk = rows * cols // 3
+    table = jnp.zeros((2 * size, 16), F32)
+    own = jnp.zeros((16, 16 * (turn + 1)), F32)
+    for i in range(3):
         place = slice(i * chunk, (i + 1) * chunk)
-        mine = rows_ref[:, place]
+        mine = flat_ref[:, place]
         rounded = mine.astype(BF16).astype(F32)
         both = jnp.concatenate([rounded, mine - rounded], 0).astype(BF16)
-        by_high = lax.dot_general(both, hi_ref[:, place], NT, preferred_element_type=F32)
-        by_low = lax.dot_general(both, lo_ref[:, place], NT, preferred_element_type=F32)
-        table = table + (by_high[0:8] + by_high[8:16] + by_low[0:8])
-        others = jnp.concatenate([ref[:, place] for ref in old_rows] + [mine], 0)
-        own = own + lax.dot_general(mine, others, NT, precision=HIGHEST, preferred_element_type=F32)
-    table = jnp.concatenate([table, jnp.zeros((8, WIDE - size), F32)], 1)
+        rows_ref[:, place] = both
+        table = table + lax.dot_general(
+            split_ref[:, place], both, NT, preferred_element_type=F32
+        )
+        others = jnp.concatenate([ref[:, place] for ref in old_rows] + [both], 0)
+        own = own + lax.dot_general(both, others, NT, preferred_element_type=F32)
+    own = [
+        own[0:8, 16 * s : 16 * s + 8]
+        + own[0:8, 16 * s + 8 : 16 * s + 16]
+        + own[8:16, 16 * s : 16 * s + 8]
+        for s in range(turn + 1)
+    ]
+    table = table[:size, 0:8] + table[:size, 8:16] + table[size:, 0:8]
+    table = jnp.concatenate([table, jnp.zeros((size, PAD - 8), F32)], 1)
+    table = jnp.transpose(jnp.concatenate([table, jnp.zeros((WIDE - size, PAD), F32)], 0))[:8]
     lane_table = lanes((8, WIDE))
     for s in range(turn + 1):
         for b in range(ORDERS):
             table = jnp.where(
-                lane_table == b * STRIDE + R + s, own[:, 8 * s + b : 8 * s + b + 1], table
+                lane_table == b * STRIDE + R + s, own[s][:, b : b + 1], table
             )
     flat = jnp.concatenate([table[a : a + 1] for a in range(ORDERS)], 1)
     for i in range(count):
@@ -570,19 +606,18 @@
 
     level = pltpu.VMEM((total, K, cols), F32)
     piece = PAD * WIDE // count
-    tall, side, coefs, hi, lo, folded = pl.pallas_call(
+    tall, side, coefs, split, folded = pl.pallas_call(
         image_body,
         out_shape=(
             shape(total, K, cols),
             shape(total, K, cols),
             shape(8, total, cols),
-            shape(size, cells, dtype=BF16),
-            shape(size, cells, dtype=BF16),
+            shape(2 * size, cells, dtype=BF16),
             shape(count, 1, piece),
         ),
         scratch_shapes=[pltpu.VMEM((total, 8, cols), F32)]
         + [level] * 6
-        + [pltpu.VMEM((size, WIDE), F32)],
+        + [pltpu.VMEM((2 * size, WIDE), F32)],
         name="images", compiler_params=LARGE,
     )(*pieces, from_left, from_right)
 
@@ -605,7 +640,7 @@
         out_shape = (
             shape(count, 1, ORDERS * WIDE),
             shape(2, total, cols),
-            shape(8, cells),
+            shape(16, cells, dtype=BF16),
             shape(rows, cols),
         ) + state_shapes
         if turn:
@@ -617,10 +652,11 @@
             out_shape=out_shape,
             scratch_shapes=[
                 pltpu.VMEM((5, 2, total, cols), F32),
-                pltpu.VMEM((ORDERS, total, cols), F32),
+                pltpu.VMEM((8, total, cols), F32),
+                pltpu.VMEM((8, cells), F32),
             ],
             name=f"turn{turn}", compiler_params=LARGE,
-        )(parts, *state, tall, side, coefs, hi, lo, *made_fields, *made_rows)
+        )(parts, *state, tall, side, coefs, split, *made_fields, *made_rows)
         made_fields.append(outs[1])
         made_rows.append(outs[2])
         made_images.append(outs[3])

time: 122 us -> 118 us (0.967)
  Pallas kernels: 42.8 us -> 37.7 us
  waiting for transfers between devices: 3.86 us -> 5.09 us
    pallas_call x3, Pallas kernels: 21 us -> 18.8 us  [local(): pl.pallas_call(functools.partial(turn_body, turn, inverse_total, count),...]
    pallas_call x1, Pallas kernels: 13.6 us -> 12 us  [local(): pl.pallas_call(image_body, out_shape=(shape(total, K, cols), shape(total,...]
    ppermute x1, waiting for transfers between devices: 2.65 us -> 3.88 us  [local(): from_right = lax.ppermute(low, 'col', down)]
    pallas_call x1, Pallas kernels: 3.56 us -> 2.33 us  [local(): pl.pallas_call(krylov_body, out_shape=shape(4 * K, PAD), name='krylov', c...]
    unnamed x6 -> x10, local copies, waits for them, and re-layouts: 3.22 us -> 3.24 us
  transfers between devices with their start and end apart: 4 -> 4, of which waited for: 2 -> 2; matrix products, arithmetic and copies ran while one was open for 0% -> 0% of each run, Pallas kernels for 3% -> 2%
where the time goes in v3:
time: 118 us
  blocking collectives  59.6 us (51%)
  Pallas kernels  37.7 us (32%)
  starting transfers between devices  10.5 us (9%)
  waiting for transfers between devices  5.09 us (4%)
  local copies, waits for them, and re-layouts  3.65 us (3%)
    all_to_all x5, blocking collectives, exchange(): return lax.all_to_all(spread, AXES, 0, 0, tiled=True)  59.6 us
    pallas_call x3, Pallas kernels, local(): pl.pallas_call(functools.partial(turn_body, turn, inverse_total, count),...  18.8 us
    pallas_call x1, Pallas kernels, local(): pl.pallas_call(image_body, out_shape=(shape(total, K, cols), shape(total,...  12 us
    ppermute x1, starting transfers between devices, local(): from_left = lax.ppermute(high, 'col', up)  4.91 us
    ppermute x1, waiting for transfers between devices, local(): from_right = lax.ppermute(low, 'col', down)  3.88 us
    unnamed x10, local copies, waits for them, and re-layouts  3.24 us
    pallas_call x1, Pallas kernels, local(): pl.pallas_call(functools.partial(final_body, inverse_total), out_shape=(s...  3.16 us
    ppermute x1, starting transfers between devices, local(): before = lax.ppermute(fields[rows - HALO:], 'row', up)  3.05 us
  transfers between devices with their start and end apart: 4, of which 2 were waited for; matrix products, arithmetic and copies ran while one was open for 0% of the time, Pallas kernels for 2%

profile of v3, /device:TPU:0, one launch (start us, length us, event | category | flops | bytes accessed | tf_op | source)
XLA Modules:
  0.0 117.5 jit_solution(5940403539332899185)
XLA Ops:
  0.6 0.0 copy-start.1
  0.7 1.5 %copy.18 = f32[37,48,128]{2,0,1:T(8,128)S(1)} copy(f32[37,48,128]{2,1,0:T(8,128)} %param.4) | data formatting | bytes 1818624 | tf_op args[0]
  2.1 0.1 pad.3.clone
  2.2 0.0 copy-done.2
  2.2 0.1 maximum_maximum_fusion.fields_ref
  2.4 0.0 copy-start
  2.4 1.3 %collective-permute-start.1 = (f32[16,40,128]{2,1,0:T(8,128)S(1)}, f32[16,40,128]{2,1,0:T(8,128)S(1)}, u32[]{:S(2)}, u32[]{:S(2)}) collective-permute-start(f32[16,40,128]{2,1,0:T(8,128)S(1)} %get-tuple-element.115), channel_id=1, source_target_pairs={{8,0},{16,8},{24,16},{9,1},{17,9},{25,17},{10,2},{18,10},{26,18},{... | collective-permute-start | bytes 983048 | tf_op jit(solution)/shard_map/ppermute | solution.py:597
  3.7 3.1 %collective-permute-start = (f32[16,40,128]{2,1,0:T(8,128)S(1)}, f32[16,40,128]{2,1,0:T(8,128)S(1)}, u32[]{:S(2)}, u32[]{:S(2)}) collective-permute-start(f32[16,40,128]{2,1,0:T(8,128)S(1)} %get-tuple-element.116), channel_id=1, source_target_pairs={{0,8},{8,16},{16,24},{1,9},{9,17},{17,25},{2,10},{10,18},{18,26},{... | collective-permute-start | bytes 983048 | tf_op jit(solution)/shard_map/ppermute | solution.py:596
  6.8 0.0 collective-permute-done.1.after_ref
  6.8 1.2 %collective-permute-done.before_ref = f32[16,40,128]{2,1,0:T(8,128)S(1)} collective-permute-done((f32[16,40,128]{2,1,0:T(8,128)S(1)}, f32[16,40,128]{2,1,0:T(8,128)S(1)}, u32[]{:S(2)}, u32[]{:S(2)}) %collective-permute-start) | collective-permute-done | bytes 327712 | tf_op jit(solution)/shard_map/ppermute | solution.py:596
  8.0 1.4 %pack.1 = (f32[10,40,128]{2,1,0:T(8,128)S(1)}, f32[10,40,128]{2,1,0:T(8,128)S(1)}) custom-call(f32[16,40,128]{2,1,0:T(8,128)S(1)} %collective-permute-done.before_ref, f32[48,40,128]{2,1,0:T(8,128)S(1)} %maximum_maximum_fusion.fields_ref, f32[16,40,128]{2,1,0:T(8,128)S(1)} %collective-permute-done.1.after_ref), custom_call_target="tpu_custom_call" | custom-call | tf_op jit(solution)/shard_map/pack/pallas_call | solution.py:600
  9.4 4.9 %collective-permute-start.2 = (f32[10,40,128]{2,1,0:T(8,128)S(1)}, f32[10,40,128]{2,1,0:T(8,128)S(1)}, u32[]{:S(2)}, u32[]{:S(2)}) collective-permute-start(f32[10,40,128]{2,1,0:T(8,128)S(1)} %get-tuple-element.55), channel_id=1, source_target_pairs={{0,1},{1,2},{2,3},{3,4},{4,5},{5,6},{6,7},{8,9},{9,10},{10,11},{11... | collective-permute-start | bytes 614408 | tf_op jit(solution)/shard_map/ppermute | solution.py:602
  14.3 1.3 %collective-permute-start.3 = (f32[10,40,128]{2,1,0:T(8,128)S(1)}, f32[10,40,128]{2,1,0:T(8,128)S(1)}, u32[]{:S(2)}, u32[]{:S(2)}) collective-permute-start(f32[10,40,128]{2,1,0:T(8,128)S(1)} %get-tuple-element.57), channel_id=1, source_target_pairs={{1,0},{2,1},{3,2},{4,3},{5,4},{6,5},{7,6},{9,8},{10,9},{11,10},{12... | collective-permute-start | bytes 614408 | tf_op jit(solution)/shard_map/ppermute | solution.py:603
  15.7 0.1 copy.14.raw_ref
  15.8 2.3 %krylov.1.refs_1_ = f32[160,128]{1,0:T(8,128)S(1)} custom-call(f32[4,37,34]{2,1,0:T(8,128)S(1)} %copy.14.raw_ref), custom_call_target="tpu_custom_call" | custom-call | tf_op jit(solution)/shard_map/krylov/pallas_call | solution.py:604
  18.1 0.0 collective-permute-done.2.left_ref
  18.1 3.9 %collective-permute-done.3.right_ref = f32[10,40,128]{2,1,0:T(8,128)S(1)} collective-permute-done((f32[10,40,128]{2,1,0:T(8,128)S(1)}, f32[10,40,128]{2,1,0:T(8,128)S(1)}, u32[]{:S(2)}, u32[]{:S(2)}) %collective-permute-start.3) | collective-permute-done | bytes 204832 | tf_op jit(solution)/shard_map/ppermute | solution.py:603
  22.0 12.0 %images.1 = (f32[80,40,128]{2,1,0:T(8,128)S(1)}, f32[80,40,128]{2,1,0:T(8,128)S(1)}, f32[8,80,128]{2,1,0:T(8,128)S(1)}, bf16[480,6144]{1,0:T(8,128)(2,1)S(1)}, f32[32,1,1024]{2,1,0:T(1,128)S(1)}) custom-call(f32[16,40,128]{2,1,0:T(8,128)S(1)} %collective-permute-done.before_ref, f32[48,40,128]{2,1,0:T(8,128)S(1)} %maximum_maximum_fusion.fields_ref, ...), custom_call_target="tpu_custom_call" | custom-call | tf_op jit(solution)/shard_map/images/pallas_call | solution.py:609
  34.0 18.1 %all_to_all.25.parts_ref = f32[32,1,1024]{2,1,0:T(1,128)S(1)} all-to-all(f32[32,1,1024]{2,1,0:T(1,128)S(1)} %get-tuple-element.58), channel_id=1, replica_groups=mesh['row'=4,'col'=8] {'row','col'}, dimensions={0} | all-to-all | bytes 262144 | tf_op jit(solution)/shard_map/all_to_all | solution.py:39
  52.1 0.1 relay.1
  52.2 10.0 %all_to_all.26.refs_0_ = f32[32,1,1024]{2,1,0:T(1,128)S(1)} all-to-all(f32[32,1,1024]{2,1,0:T(1,128)S(1)} %relay.1), channel_id=1, replica_groups=mesh['row'=4,'col'=8] {'row','col'}, dimensions={0} | all-to-all | bytes 262144 | tf_op jit(solution)/shard_map/all_to_all | solution.py:39
  62.1 6.7 %turn0.1 = (f32[32,1,1280]{2,1,0:T(1,128)S(1)}, f32[2,80,128]{2,1,0:T(8,128)S(1)}, bf16[16,6144]{1,0:T(8,128)(2,1)S(1)}, f32[48,128]{1,0:T(8,128)S(1)}, f32[40,2...) custom-call(f32[32,1,1024]{2,1,0:T(1,128)S(1)} %all_to_all.26.refs_0, ...), custom_call_target="tpu_custom_call" | custom-call | tf_op jit(solution)/shard_map/turn0/pallas_call | solution.py:650
  68.9 10.2 %all_to_all.27.refs_0_ = f32[32,1,1280]{2,1,0:T(1,128)S(1)} all-to-all(f32[32,1,1280]{2,1,0:T(1,128)S(1)} %get-tuple-element.64), channel_id=1, replica_groups=mesh['row'=4,'col'=8] {'row','col'}, dimensions={0} | all-to-all | bytes 327680 | tf_op jit(solution)/shard_map/all_to_all | solution.py:39
  79.0 5.8 %turn1.1 = (f32[32,1,1280]{2,1,0:T(1,128)S(1)}, f32[2,80,128]{2,1,0:T(8,128)S(1)}, bf16[16,6144]{1,0:T(8,128)(2,1)S(1)}, f32[48,128]{1,0:T(8,128)S(1)}, f32[40,2...) custom-call(f32[32,1,1280]{2,1,0:T(1,128)S(1)} %all_to_all.27.refs_0, ...), custom_call_target="tpu_custom_call" | custom-call | tf_op jit(solution)/shard_map/turn1/pallas_call | solution.py:650
  84.8 10.7 %all_to_all.28.refs_0_ = f32[32,1,1280]{2,1,0:T(1,128)S(1)} all-to-all(f32[32,1,1280]{2,1,0:T(1,128)S(1)} %get-tuple-element.73), channel_id=1, replica_groups=mesh['row'=4,'col'=8] {'row','col'}, dimensions={0} | all-to-all | bytes 327680 | tf_op jit(solution)/shard_map/all_to_all | solution.py:39
  95.5 6.3 %turn2.1 = (f32[32,1,1280]{2,1,0:T(1,128)S(1)}, f32[2,80,128]{2,1,0:T(8,128)S(1)}, bf16[16,6144]{1,0:T(8,128)(2,1)}, f32[48,128]{1,0:T(8,128)S(1)}, f32[40,256]{...) custom-call(f32[32,1,1280]{2,1,0:T(1,128)S(1)} %all_to_all.28.refs_0, ...), custom_call_target="tpu_custom_call" | custom-call | tf_op jit(solution)/shard_map/turn2/pallas_call | solution.py:650
  101.8 10.7 %all_to_all.29.refs_0_ = f32[32,1,1280]{2,1,0:T(1,128)S(1)} all-to-all(f32[32,1,1280]{2,1,0:T(1,128)S(1)} %get-tuple-element.82), channel_id=1, replica_groups=mesh['row'=4,'col'=8] {'row','col'}, dimensions={0} | all-to-all | bytes 327680 | tf_op jit(solution)/shard_map/all_to_all | solution.py:39
  112.4 3.2 %final.1 = (f32[3,48,128]{2,1,0:T(8,128)}, f32[4,40,37]{2,1,0:T(8,128)S(1)}, f32[3,37]{1,0:T(4,128)}, f32[256,256]{1,0:T(8,128)S(1)}, f32[3,48,128]{2,1,0:T(8,128)}) custom-call(f32[32,1,1280]{2,1,0:T(1,128)S(1)} %all_to_all.29.refs_0_, f32[40,256]{1,0:T(8,128)S(1)} %get-tuple-element.83.refs_1_, f32[40,128]{1,0:T(8,128)S(1)} %get-tuple-element.84.refs_2_, ...), custom_call_target="tpu_custom_call" | custom-call | tf_op jit(solution)/shard_map/final/pallas_call | solution.py:672
  115.6 0.7 copy.15
  116.3 0.2 reshape.13
  116.6 0.1 slice.18
  116.6 0.9 copy.16
  (5 shorter events, 0.1 us)
Async XLA Ops:
  0.6 1.6 %copy-start.1 = (f32[48,128]{1,0:T(8,128)S(1)}, f32[48,128]{1,0:T(8,128)}, u32[]{:S(2)}) copy-start(f32[48,128]{1,0:T(8,128)} %param.7) | copy-start | bytes 73732
  0.6 1.6 %copy-start.2 = (f32[48,128]{1,0:T(8,128)S(1)}, f32[48,128]{1,0:T(8,128)}, u32[]{:S(2)}) copy-start(f32[48,128]{1,0:T(8,128)} %param.6) | copy-start | bytes 73732
  2.4 13.3 %copy-start = (f32[4,37,34]{1,0,2:T(4,128)S(1)}, f32[4,37,34]{1,0,2:T(4,128)}, u32[]{:S(2)}) copy-start(f32[4,37,34]{1,0,2:T(4,128)} %param.5) | copy-start | bytes 60388
  2.4 4.4 %collective-permute-start.1 = (f32[16,40,128]{2,1,0:T(8,128)S(1)}, f32[16,40,128]{2,1,0:T(8,128)S(1)}, u32[]{:S(2)}, u32[]{:S(2)}) collective-permute-start(f32[16,40,128]{2,1,0:T(8,128)S(1)} %get-tuple-element.115), channel_id=1, source_target_pairs={{8,0},{16,8},{24,16},{9,1},{17,9},{25,17},{10,2},{18,10},{26,18},{... | collective-permute-start | bytes 983048 | tf_op jit(solution)/shard_map/ppermute | solution.py:597
  3.7 4.3 %collective-permute-start = (f32[16,40,128]{2,1,0:T(8,128)S(1)}, f32[16,40,128]{2,1,0:T(8,128)S(1)}, u32[]{:S(2)}, u32[]{:S(2)}) collective-permute-start(f32[16,40,128]{2,1,0:T(8,128)S(1)} %get-tuple-element.116), channel_id=1, source_target_pairs={{0,8},{8,16},{16,24},{1,9},{9,17},{17,25},{2,10},{10,18},{18,26},{... | collective-permute-start | bytes 983048 | tf_op jit(solution)/shard_map/ppermute | solution.py:596
  9.4 8.7 %collective-permute-start.2 = (f32[10,40,128]{2,1,0:T(8,128)S(1)}, f32[10,40,128]{2,1,0:T(8,128)S(1)}, u32[]{:S(2)}, u32[]{:S(2)}) collective-permute-start(f32[10,40,128]{2,1,0:T(8,128)S(1)} %get-tuple-element.55), channel_id=1, source_target_pairs={{0,1},{1,2},{2,3},{3,4},{4,5},{5,6},{6,7},{8,9},{9,10},{10,11},{11... | collective-permute-start | bytes 614408 | tf_op jit(solution)/shard_map/ppermute | solution.py:602
  14.3 7.7 %collective-permute-start.3 = (f32[10,40,128]{2,1,0:T(8,128)S(1)}, f32[10,40,128]{2,1,0:T(8,128)S(1)}, u32[]{:S(2)}, u32[]{:S(2)}) collective-permute-start(f32[10,40,128]{2,1,0:T(8,128)S(1)} %get-tuple-element.57), channel_id=1, source_target_pairs={{1,0},{2,1},{3,2},{4,3},{5,4},{6,5},{7,6},{9,8},{10,9},{11,10},{12... | collective-permute-start | bytes 614408 | tf_op jit(solution)/shard_map/ppermute | solution.py:603

commit v4 on v3

--- a/solution.py
+++ b/solution.py
@@ -23,7 +23,8 @@
 HALO = (ORDERS - 1) * (STEPS + 1)
 STRIDE = 48
 WIDE = 256
-UNROLL = 4
+UNROLL = 24
+GROUPS = 2
 SMALL = pltpu.CompilerParams(vmem_limit_bytes=8 << 20)
 LARGE = pltpu.CompilerParams(vmem_limit_bytes=24 << 20)
 PAD = 128
@@ -418,19 +419,26 @@
     raw_only = sublanes((K, cols)) < R
     weights = [jnp.where(raw_only, upright[:K, j : j + 1], 0.0) for j in range(5)]
 
-    def mix(g, carry):
-        lists = [[[], []] for _ in range(5)]
-        for k in range(8):
-            for half, ref in enumerate((main_ref, side_ref)):
+    def mix_group(g):
+        for half, ref in enumerate((main_ref, side_ref)):
+            lists = [[] for _ in range(5)]
+            for k in range(8):
                 cells = ref[g * 8 + k]
                 for j in range(5):
-                    lists[j][half].append(jnp.sum(weights[j] * cells, axis=0, keepdims=True))
-        for j in range(5):
-            for half in range(2):
-                z_ref[j, half, pl.ds(pl.multiple_of(g * 8, 8), 8), :] = jnp.concatenate(lists[j][half], 0)
+                    lists[j].append(jnp.sum(weights[j] * cells, axis=0, keepdims=True))
+            for j in range(5):
+                z_ref[j, half, pl.ds(pl.multiple_of(g * 8, 8), 8), :] = jnp.concatenate(lists[j], 0)
+
+    def mix(i, carry):
+        for k in range(GROUPS):
+            mix_group(idle + i * GROUPS + k)
         return carry
 
-    lax.fori_loop(0, total // 8, mix, 0)
+    idle = (ORDERS - 1) * turn // 8
+    if idle:
+        z_ref[:, :, : 8 * idle] = jnp.zeros((5, 2, 8 * idle, cols), F32)
+        z_ref[:, :, total - 8 * idle :] = jnp.zeros((5, 2, 8 * idle, cols), F32)
+    lax.fori_loop(0, (total // 8 - 2 * idle) // GROUPS, mix, 0)
 
     z = []
     for j in range(5):
@@ -529,8 +537,10 @@
     state = tuple(r[...] for r in state_refs[:5]) + (state_refs[5][:, 0:1],)
     state, table, sigma, hessenberg = absorb(parts_ref[...], state, STEPS - 1, inverse_total)
     factor = state[1]
+    flat = jnp.concatenate([state[4], jnp.zeros((WIDE - 4 * K, PAD), F32)], 0)
+    flat = jnp.transpose(flat)[:WIDTH]
     for j in range(4):
-        coefficients_ref[j] = state[4][j * K : (j + 1) * K, :WIDTH]
+        coefficients_ref[:, j, :] = flat[:, j * K : (j + 1) * K]
     hessenberg_ref[...] = jnp.concatenate([r[0:1] for r in old_hessen] + [hessenberg], 0)[:, :WIDTH]
     sigmas = [ref[0:1, 0:1] for ref in old_sigmas] + [sigma]
     rows = columns_ref.shape[1]
@@ -567,7 +577,10 @@
     blocks = [padded] + [pltpu.roll(padded, a * STRIDE, 1) for a in range(1, ORDERS)]
     diagonal = jnp.concatenate(blocks + [jnp.zeros((WIDE - ORDERS * STRIDE, WIDE), F32)], 0)
     half = jnp.dot(diagonal, whole, precision=HIGHEST, preferred_element_type=F32)
-    gram_ref[...] = lax.dot_general(half, diagonal, NT, precision=HIGHEST, preferred_element_type=F32)
+    done = lax.dot_general(half, diagonal, NT, precision=HIGHEST, preferred_element_type=F32)
+    for a in range(ORDERS):
+        for b in range(ORDERS):
+            gram_ref[a, b] = done[a * STRIDE : a * STRIDE + K, b * STRIDE : b * STRIDE + K]
 
 
 def shape(*dims, dtype=F32):
@@ -673,14 +686,15 @@
         functools.partial(final_body, inverse_total),
         out_shape=(
             shape(STEPS, rows, cols),
-            shape(4, K, WIDTH),
+            shape(WIDTH, 4, K),
             shape(STEPS, WIDTH),
-            shape(WIDE, WIDE),
+            shape(ORDERS, ORDERS, K, K),
             shape(STEPS, rows, cols),
         ),
         name="final", compiler_params=SMALL,
     )(parts, *state, folded, *tables, *sigmas, *hessen, *made_fields, *made_images)
-    gram = gram[:size, :size].reshape(ORDERS, STRIDE, ORDERS, STRIDE)[:, :K, :, :K]
+    gram = jnp.transpose(gram, (0, 2, 1, 3))
+    coefficients = jnp.transpose(coefficients, (1, 2, 0))
     return (new_columns, coefficients, hessenberg, gram, new_images)
 
 

time: 118 us -> 113 us (0.958)
  Pallas kernels: 37.7 us -> 34.6 us
  local copies, waits for them, and re-layouts: 3.65 us -> 1.74 us
    pallas_call x1, Pallas kernels: 12 us -> 8.79 us  [local(): pl.pallas_call(image_body, out_shape=(shape(total, K, cols), shape(total,...]
    unnamed x10 -> x8, local copies, waits for them, and re-layouts: 3.24 us -> 1.62 us
where the time goes in v4:
time: 113 us; the launch traced here: 112 us
  blocking collectives  59.6 us (53%)
  Pallas kernels  34.6 us (31%)
  starting transfers between devices  10.5 us (9%)
  waiting for transfers between devices  5.09 us (5%)
  local copies, waits for them, and re-layouts  1.74 us (2%)
    all_to_all x5, blocking collectives, exchange(): return lax.all_to_all(spread, AXES, 0, 0, tiled=True)  59.6 us
    pallas_call x3, Pallas kernels, local(): pl.pallas_call(functools.partial(turn_body, turn, inverse_total, count),...  18.3 us
    pallas_call x1, Pallas kernels, local(): pl.pallas_call(image_body, out_shape=(shape(total, K, cols), shape(total,...  8.79 us
    ppermute x1, starting transfers between devices, local(): from_left = lax.ppermute(high, 'col', up)  4.91 us
    ppermute x1, waiting for transfers between devices, local(): from_right = lax.ppermute(low, 'col', down)  3.88 us
    pallas_call x1, Pallas kernels, local(): pl.pallas_call(functools.partial(final_body, inverse_total), out_shape=(s...  3.69 us
    ppermute x1, starting transfers between devices, local(): before = lax.ppermute(fields[rows - HALO:], 'row', up)  3.05 us
    pallas_call x1, Pallas kernels, local(): pl.pallas_call(krylov_body, out_shape=shape(4 * K, PAD), name='krylov', c...  2.33 us
  transfers between devices with their start and end apart: 4, of which 2 were waited for; matrix products, arithmetic and copies ran while one was open for 0% of the time, Pallas kernels for 2%

profile of v4, /device:TPU:0, one launch (start us, length us, event | category | flops | bytes accessed | tf_op | source)
XLA Modules:
  0.0 112.4 jit_solution(13902258231137265727)
XLA Ops:
  0.6 0.0 copy-start.1
  0.6 0.0 copy-start.2
  0.7 1.5 %copy.12 = f32[37,48,128]{2,0,1:T(8,128)S(1)} copy(f32[37,48,128]{2,1,0:T(8,128)} %param.4) | data formatting | bytes 1818624 | tf_op args[0]
  2.1 0.1 pad.3.clone
  2.2 0.0 copy-done.1
  2.2 0.0 copy-done.2
  2.2 0.1 maximum_maximum_fusion.fields_ref
  2.4 0.0 copy-start
  2.4 1.3 %collective-permute-start.1 = (f32[16,40,128]{2,1,0:T(8,128)S(1)}, f32[16,40,128]{2,1,0:T(8,128)S(1)}, u32[]{:S(2)}, u32[]{:S(2)}) collective-permute-start(f32[16,40,128]{2,1,0:T(8,128)S(1)} %get-tuple-element.105), channel_id=1, source_target_pairs={{8,0},{16,8},{24,16},{9,1},{17,9},{25,17},{10,2},{18,10},{26,18},{... | collective-permute-start | bytes 983048 | tf_op jit(solution)/shard_map/ppermute | solution.py:610
  3.7 3.1 %collective-permute-start = (f32[16,40,128]{2,1,0:T(8,128)S(1)}, f32[16,40,128]{2,1,0:T(8,128)S(1)}, u32[]{:S(2)}, u32[]{:S(2)}) collective-permute-start(f32[16,40,128]{2,1,0:T(8,128)S(1)} %get-tuple-element.106), channel_id=1, source_target_pairs={{0,8},{8,16},{16,24},{1,9},{9,17},{17,25},{2,10},{10,18},{18,26},{... | collective-permute-start | bytes 983048 | tf_op jit(solution)/shard_map/ppermute | solution.py:609
  6.8 0.0 collective-permute-done.1.after_ref
  6.8 1.2 %collective-permute-done.before_ref = f32[16,40,128]{2,1,0:T(8,128)S(1)} collective-permute-done((f32[16,40,128]{2,1,0:T(8,128)S(1)}, f32[16,40,128]{2,1,0:T(8,128)S(1)}, u32[]{:S(2)}, u32[]{:S(2)}) %collective-permute-start) | collective-permute-done | bytes 327712 | tf_op jit(solution)/shard_map/ppermute | solution.py:609
  8.0 1.4 %pack.1 = (f32[10,40,128]{2,1,0:T(8,128)S(1)}, f32[10,40,128]{2,1,0:T(8,128)S(1)}) custom-call(f32[16,40,128]{2,1,0:T(8,128)S(1)} %collective-permute-done.before_ref, f32[48,40,128]{2,1,0:T(8,128)S(1)} %maximum_maximum_fusion.fields_ref, f32[16,40,128]{2,1,0:T(8,128)S(1)} %collective-permute-done.1.after_ref), custom_call_target="tpu_custom_call" | custom-call | tf_op jit(solution)/shard_map/pack/pallas_call | solution.py:613
  9.4 4.9 %collective-permute-start.2 = (f32[10,40,128]{2,1,0:T(8,128)S(1)}, f32[10,40,128]{2,1,0:T(8,128)S(1)}, u32[]{:S(2)}, u32[]{:S(2)}) collective-permute-start(f32[10,40,128]{2,1,0:T(8,128)S(1)} %get-tuple-element.55), channel_id=1, source_target_pairs={{0,1},{1,2},{2,3},{3,4},{4,5},{5,6},{6,7},{8,9},{9,10},{10,11},{11... | collective-permute-start | bytes 614408 | tf_op jit(solution)/shard_map/ppermute | solution.py:615
  14.3 1.3 %collective-permute-start.3 = (f32[10,40,128]{2,1,0:T(8,128)S(1)}, f32[10,40,128]{2,1,0:T(8,128)S(1)}, u32[]{:S(2)}, u32[]{:S(2)}) collective-permute-start(f32[10,40,128]{2,1,0:T(8,128)S(1)} %get-tuple-element.57), channel_id=1, source_target_pairs={{1,0},{2,1},{3,2},{4,3},{5,4},{6,5},{7,6},{9,8},{10,9},{11,10},{12... | collective-permute-start | bytes 614408 | tf_op jit(solution)/shard_map/ppermute | solution.py:616
  15.6 0.0 copy-done
  15.7 0.1 copy.10.raw_ref
  15.8 2.3 %krylov.1.refs_1_ = f32[160,128]{1,0:T(8,128)S(1)} custom-call(f32[4,37,34]{2,1,0:T(8,128)S(1)} %copy.10.raw_ref), custom_call_target="tpu_custom_call" | custom-call | tf_op jit(solution)/shard_map/krylov/pallas_call | solution.py:617
  18.1 0.0 collective-permute-done.2.left_ref
  18.1 3.9 %collective-permute-done.3.right_ref = f32[10,40,128]{2,1,0:T(8,128)S(1)} collective-permute-done((f32[10,40,128]{2,1,0:T(8,128)S(1)}, f32[10,40,128]{2,1,0:T(8,128)S(1)}, u32[]{:S(2)}, u32[]{:S(2)}) %collective-permute-start.3) | collective-permute-done | bytes 204832 | tf_op jit(solution)/shard_map/ppermute | solution.py:616
  22.0 8.8 %images.1 = (f32[80,40,128]{2,1,0:T(8,128)S(1)}, f32[80,40,128]{2,1,0:T(8,128)S(1)}, f32[8,80,128]{2,1,0:T(8,128)S(1)}, bf16[480,6144]{1,0:T(8,128)(2,1)S(1)}, f32[32,1,1024]{2,1,0:T(1,128)S(1)}) custom-call(f32[16,40,128]{2,1,0:T(8,128)S(1)} %collective-permute-done.before_ref, f32[48,40,128]{2,1,0:T(8,128)S(1)} %maximum_maximum_fusion.fields_ref, ...), custom_call_target="tpu_custom_call" | custom-call | tf_op jit(solution)/shard_map/images/pallas_call | solution.py:622
  30.8 18.1 %all_to_all.25.parts_ref = f32[32,1,1024]{2,1,0:T(1,128)S(1)} all-to-all(f32[32,1,1024]{2,1,0:T(1,128)S(1)} %get-tuple-element.58), channel_id=1, replica_groups=mesh['row'=4,'col'=8] {'row','col'}, dimensions={0} | all-to-all | bytes 262144 | tf_op jit(solution)/shard_map/all_to_all | solution.py:40
  48.9 0.1 relay.1
  49.0 10.0 %all_to_all.26.refs_0_ = f32[32,1,1024]{2,1,0:T(1,128)S(1)} all-to-all(f32[32,1,1024]{2,1,0:T(1,128)S(1)} %relay.1), channel_id=1, replica_groups=mesh['row'=4,'col'=8] {'row','col'}, dimensions={0} | all-to-all | bytes 262144 | tf_op jit(solution)/shard_map/all_to_all | solution.py:40
  59.0 6.7 %turn0.1 = (f32[32,1,1280]{2,1,0:T(1,128)S(1)}, f32[2,80,128]{2,1,0:T(8,128)S(1)}, bf16[16,6144]{1,0:T(8,128)(2,1)S(1)}, f32[48,128]{1,0:T(8,128)S(1)}, f32[40,2...) custom-call(f32[32,1,1024]{2,1,0:T(1,128)S(1)} %all_to_all.26.refs_0, ...), custom_call_target="tpu_custom_call" | custom-call | tf_op jit(solution)/shard_map/turn0/pallas_call | solution.py:663
  65.6 10.2 %all_to_all.27.refs_0_ = f32[32,1,1280]{2,1,0:T(1,128)S(1)} all-to-all(f32[32,1,1280]{2,1,0:T(1,128)S(1)} %get-tuple-element.64), channel_id=1, replica_groups=mesh['row'=4,'col'=8] {'row','col'}, dimensions={0} | all-to-all | bytes 327680 | tf_op jit(solution)/shard_map/all_to_all | solution.py:40
  75.8 5.7 %turn1.1 = (f32[32,1,1280]{2,1,0:T(1,128)S(1)}, f32[2,80,128]{2,1,0:T(8,128)S(1)}, bf16[16,6144]{1,0:T(8,128)(2,1)S(1)}, f32[48,128]{1,0:T(8,128)S(1)}, f32[40,2...) custom-call(f32[32,1,1280]{2,1,0:T(1,128)S(1)} %all_to_all.27.refs_0, ...), custom_call_target="tpu_custom_call" | custom-call | tf_op jit(solution)/shard_map/turn1/pallas_call | solution.py:663
  81.5 10.7 %all_to_all.28.refs_0_ = f32[32,1,1280]{2,1,0:T(1,128)S(1)} all-to-all(f32[32,1,1280]{2,1,0:T(1,128)S(1)} %get-tuple-element.73), channel_id=1, replica_groups=mesh['row'=4,'col'=8] {'row','col'}, dimensions={0} | all-to-all | bytes 327680 | tf_op jit(solution)/shard_map/all_to_all | solution.py:40
  92.2 5.9 %turn2.1 = (f32[32,1,1280]{2,1,0:T(1,128)S(1)}, f32[2,80,128]{2,1,0:T(8,128)S(1)}, bf16[16,6144]{1,0:T(8,128)(2,1)}, f32[48,128]{1,0:T(8,128)S(1)}, f32[40,256]{...) custom-call(f32[32,1,1280]{2,1,0:T(1,128)S(1)} %all_to_all.28.refs_0, ...), custom_call_target="tpu_custom_call" | custom-call | tf_op jit(solution)/shard_map/turn2/pallas_call | solution.py:663
  98.1 10.7 %all_to_all.29.refs_0_ = f32[32,1,1280]{2,1,0:T(1,128)S(1)} all-to-all(f32[32,1,1280]{2,1,0:T(1,128)S(1)} %get-tuple-element.82), channel_id=1, replica_groups=mesh['row'=4,'col'=8] {'row','col'}, dimensions={0} | all-to-all | bytes 327680 | tf_op jit(solution)/shard_map/all_to_all | solution.py:40
  108.8 3.7 %final.1 = (f32[3,48,128]{2,1,0:T(8,128)}, f32[37,4,40]{2,1,0:T(4,128)}, f32[3,37]{1,0:T(4,128)}, f32[5,5,40,40]{3,2,1,0:T(8,128)}, f32[3,48,128]{2,1,0:T(8,128)}) custom-call(f32[32,1,1280]{2,1,0:T(1,128)S(1)} %all_to_all.29.refs_0_, f32[40,256]{1,0:T(8,128)S(1)} %get-tuple-element.83.refs_1_, f32[40,128]{1,0:T(8,128)S(1)} %get-tuple-element.84.refs_2_, ...), custom_call_target="tpu_custom_call" | custom-call | tf_op jit(solution)/shard_map/final/pallas_call | solution.py:685
  (1 shorter events, 0.0 us)
Async XLA Ops:
  0.6 1.6 %copy-start.1 = (f32[48,128]{1,0:T(8,128)S(1)}, f32[48,128]{1,0:T(8,128)}, u32[]{:S(2)}) copy-start(f32[48,128]{1,0:T(8,128)} %param.7) | copy-start | bytes 73732
  0.6 1.6 %copy-start.2 = (f32[48,128]{1,0:T(8,128)S(1)}, f32[48,128]{1,0:T(8,128)}, u32[]{:S(2)}) copy-start(f32[48,128]{1,0:T(8,128)} %param.6) | copy-start | bytes 73732
  2.4 13.3 %copy-start = (f32[4,37,34]{1,0,2:T(4,128)S(1)}, f32[4,37,34]{1,0,2:T(4,128)}, u32[]{:S(2)}) copy-start(f32[4,37,34]{1,0,2:T(4,128)} %param.5) | copy-start | bytes 60388
  2.4 4.4 %collective-permute-start.1 = (f32[16,40,128]{2,1,0:T(8,128)S(1)}, f32[16,40,128]{2,1,0:T(8,128)S(1)}, u32[]{:S(2)}, u32[]{:S(2)}) collective-permute-start(f32[16,40,128]{2,1,0:T(8,128)S(1)} %get-tuple-element.105), channel_id=1, source_target_pairs={{8,0},{16,8},{24,16},{9,1},{17,9},{25,17},{10,2},{18,10},{26,18},{... | collective-permute-start | bytes 983048 | tf_op jit(solution)/shard_map/ppermute | solution.py:610
  3.7 4.3 %collective-permute-start = (f32[16,40,128]{2,1,0:T(8,128)S(1)}, f32[16,40,128]{2,1,0:T(8,128)S(1)}, u32[]{:S(2)}, u32[]{:S(2)}) collective-permute-start(f32[16,40,128]{2,1,0:T(8,128)S(1)} %get-tuple-element.106), channel_id=1, source_target_pairs={{0,8},{8,16},{16,24},{1,9},{9,17},{17,25},{2,10},{10,18},{18,26},{... | collective-permute-start | bytes 983048 | tf_op jit(solution)/shard_map/ppermute | solution.py:609
  9.4 8.7 %collective-permute-start.2 = (f32[10,40,128]{2,1,0:T(8,128)S(1)}, f32[10,40,128]{2,1,0:T(8,128)S(1)}, u32[]{:S(2)}, u32[]{:S(2)}) collective-permute-start(f32[10,40,128]{2,1,0:T(8,128)S(1)} %get-tuple-element.55), channel_id=1, source_target_pairs={{0,1},{1,2},{2,3},{3,4},{4,5},{5,6},{6,7},{8,9},{9,10},{10,11},{11... | collective-permute-start | bytes 614408 | tf_op jit(solution)/shard_map/ppermute | solution.py:615
  14.3 7.7 %collective-permute-start.3 = (f32[10,40,128]{2,1,0:T(8,128)S(1)}, f32[10,40,128]{2,1,0:T(8,128)S(1)}, u32[]{:S(2)}, u32[]{:S(2)}) collective-permute-start(f32[10,40,128]{2,1,0:T(8,128)S(1)} %get-tuple-element.57), channel_id=1, source_target_pairs={{1,0},{2,1},{3,2},{4,3},{5,4},{6,5},{7,6},{9,8},{10,9},{11,10},{12... | collective-permute-start | bytes 614408 | tf_op jit(solution)/shard_map/ppermute | solution.py:616

commit v5 on v4

--- a/solution.py
+++ b/solution.py
@@ -23,8 +23,6 @@
 HALO = (ORDERS - 1) * (STEPS + 1)
 STRIDE = 48
 WIDE = 256
-UNROLL = 24
-GROUPS = 2
 SMALL = pltpu.CompilerParams(vmem_limit_bytes=8 << 20)
 LARGE = pltpu.CompilerParams(vmem_limit_bytes=24 << 20)
 PAD = 128
@@ -76,9 +74,12 @@
         return carry
 
     last = edge + rows // span
-    lax.fori_loop(0, edge, functools.partial(group, before_ref, 0), 0)
-    lax.fori_loop(edge, last, functools.partial(group, fields_ref, edge), 0)
-    lax.fori_loop(last, last + edge, functools.partial(group, after_ref, last), 0)
+    for g in range(0, edge):
+        group(before_ref, 0, g, 0)
+    for g in range(edge, last):
+        group(fields_ref, edge, g, 0)
+    for g in range(last, last + edge):
+        group(after_ref, last, g, 0)
 
 
 def lower_inverse(matrix, count):
@@ -189,9 +190,12 @@
 
     first = HALO // span
     last = first + rows // span
-    lax.fori_loop(0, first, functools.partial(unpack, before_ref, 0), 0)
-    lax.fori_loop(first, last, functools.partial(unpack, fields_ref, first), 0)
-    lax.fori_loop(last, last + first, functools.partial(unpack, after_ref, last), 0)
+    for g in range(0, first):
+        unpack(before_ref, 0, g, 0)
+    for g in range(first, last):
+        unpack(fields_ref, first, g, 0)
+    for g in range(last, last + first):
+        unpack(after_ref, last, g, 0)
 
     blank = jnp.zeros((STRIDE - slots, cols), F32)
     size = ORDERS * STRIDE
@@ -200,7 +204,7 @@
         whole = jnp.concatenate([cells, blank], 0)
         high = whole.astype(BF16)
         low = (whole - high.astype(F32)).astype(BF16)
-        place = pl.ds(pl.multiple_of((r - HALO) * cols, cols), cols)
+        place = slice((r - HALO) * cols, (r - HALO + 1) * cols)
         split_ref[order * STRIDE : (order + 1) * STRIDE, place] = high
         split_ref[size + order * STRIDE : size + (order + 1) * STRIDE, place] = low
 
@@ -241,22 +245,14 @@
 
         reach = ORDERS - 1 - order
 
-        def inner(i, carry):
-            for k in range(UNROLL):
-                one(HALO + i * UNROLL + k, True)
-            return carry
-
         for k in range(reach):
             one(HALO - 1 - k, False)
             one(HALO + rows + k, False)
-        lax.fori_loop(0, rows // UNROLL, inner, 0)
-
-    def plain(i, carry):
-        for k in range(UNROLL):
-            keep(0, HALO + i * UNROLL + k, tall_ref[HALO + i * UNROLL + k])
-        return carry
-
-    lax.fori_loop(0, rows // UNROLL, plain, 0)
+        for r in range(HALO, HALO + rows):
+            one(r, True)
+
+    for r in range(HALO, HALO + rows):
+        keep(0, r, tall_ref[r])
     level(1, (tall_ref, side_ref), None, (m1, s1), True)
     level(2, (m1, s1), (tall_ref, side_ref), (m2, s2), True)
     level(3, (m2, s2), (m1, s1), (m3, s3), True)
@@ -290,10 +286,11 @@
     for i in range(3):
         acc_ref[i * K : (i + 1) * K, :] = bands[i]
     count, _, piece = gram_ref.shape
-    deep = piece // WIDE
+    width = min(piece, WIDE)
     for i in range(count):
-        for k in range(deep):
-            gram_ref[i, :, k * WIDE : (k + 1) * WIDE] = acc_ref[i * deep + k : i * deep + k + 1, :]
+        for k in range(0, piece, width):
+            spot, start = divmod(i * piece + k, WIDE)
+            gram_ref[i, :, k : k + width] = acc_ref[spot : spot + 1, start : start + width]
 
 
 def relay_body(parts_ref, spread_ref):
@@ -395,11 +392,12 @@
         hessenberg_ref[...] = jnp.broadcast_to(hessenberg, hessenberg_ref.shape)
     else:
         pieces, _, piece = parts_ref.shape
-        deep = piece // WIDE
+        width = min(piece, WIDE)
         for i in range(pieces):
-            for k in range(deep):
-                folded_ref[i * deep + k : i * deep + k + 1, :] = (
-                    parts_ref[i, :, k * WIDE : (k + 1) * WIDE] * inverse_total
+            for k in range(0, piece, width):
+                spot, start = divmod(i * piece + k, WIDE)
+                folded_ref[spot : spot + 1, start : start + width] = (
+                    parts_ref[i, :, k : k + width] * inverse_total
                 )
         gram = folded_ref[0:K, :]
         diagonal = lanes((K, PAD)) == sublanes((K, PAD))
@@ -430,15 +428,16 @@
                 z_ref[j, half, pl.ds(pl.multiple_of(g * 8, 8), 8), :] = jnp.concatenate(lists[j], 0)
 
     def mix(i, carry):
-        for k in range(GROUPS):
-            mix_group(idle + i * GROUPS + k)
+        for k in range(groups):
+            mix_group(idle + i * groups + k)
         return carry
 
     idle = (ORDERS - 1) * turn // 8
+    groups = (total // 8 - 2 * idle) // 2
     if idle:
         z_ref[:, :, : 8 * idle] = jnp.zeros((5, 2, 8 * idle, cols), F32)
         z_ref[:, :, total - 8 * idle :] = jnp.zeros((5, 2, 8 * idle, cols), F32)
-    lax.fori_loop(0, (total // 8 - 2 * idle) // GROUPS, mix, 0)
+    lax.fori_loop(0, 2, mix, 0)
 
     z = []
     for j in range(5):

time: 113 us -> 110 us (0.973)
  Pallas kernels: 34.6 us -> 32 us
    pallas_call x1, Pallas kernels: 8.79 us -> 6.9 us  [local(): pl.pallas_call(image_body, out_shape=(shape(total, K, cols), shape(total,...]
where the time goes in v5:
time: 110 us
  blocking collectives  59.6 us (54%)
  Pallas kernels  32 us (29%)
  starting transfers between devices  10.5 us (10%)
  waiting for transfers between devices  5.09 us (5%)
  local copies, waits for them, and re-layouts  1.74 us (2%)
    all_to_all x5, blocking collectives, exchange(): return lax.all_to_all(spread, AXES, 0, 0, tiled=True)  59.6 us
    pallas_call x3, Pallas kernels, local(): pl.pallas_call(functools.partial(turn_body, turn, inverse_total, count),...  18.2 us
    pallas_call x1, Pallas kernels, local(): pl.pallas_call(image_body, out_shape=(shape(total, K, cols), shape(total,...  6.9 us
    ppermute x1, starting transfers between devices, local(): from_left = lax.ppermute(high, 'col', up)  4.91 us
    ppermute x1, waiting for transfers between devices, local(): from_right = lax.ppermute(low, 'col', down)  3.88 us
    pallas_call x1, Pallas kernels, local(): pl.pallas_call(functools.partial(final_body, inverse_total), out_shape=(s...  3.69 us
    ppermute x1, starting transfers between devices, local(): before = lax.ppermute(fields[rows - HALO:], 'row', up)  3.05 us
    pallas_call x1, Pallas kernels, local(): pl.pallas_call(krylov_body, out_shape=shape(4 * K, PAD), name='krylov', c...  2.32 us
  transfers between devices with their start and end apart: 4, of which 2 were waited for; matrix products, arithmetic and copies ran while one was open for 0% of the time, Pallas kernels for 2%

profile of v5, /device:TPU:0, one launch (start us, length us, event | category | flops | bytes accessed | tf_op | source)
XLA Modules:
  0.0 109.9 jit_solution(18112061647787378057)
XLA Ops:
  0.6 0.0 copy-start.1
  0.6 0.0 copy-start.2
  0.7 1.5 %copy.12 = f32[37,48,128]{2,0,1:T(8,128)S(1)} copy(f32[37,48,128]{2,1,0:T(8,128)} %param.4) | data formatting | bytes 1818624 | tf_op args[0]
  2.1 0.1 pad.3.clone
  2.2 0.0 copy-done.1
  2.2 0.0 copy-done.2
  2.2 0.1 maximum_maximum_fusion.fields_ref
  2.4 0.0 copy-start
  2.4 1.3 %collective-permute-start.1 = (f32[16,40,128]{2,1,0:T(8,128)S(1)}, f32[16,40,128]{2,1,0:T(8,128)S(1)}, u32[]{:S(2)}, u32[]{:S(2)}) collective-permute-start(f32[16,40,128]{2,1,0:T(8,128)S(1)} %get-tuple-element.105), channel_id=1, source_target_pairs={{8,0},{16,8},{24,16},{9,1},{17,9},{25,17},{10,2},{18,10},{26,18},{... | collective-permute-start | bytes 983048 | tf_op jit(solution)/shard_map/ppermute | solution.py:609
  3.7 3.1 %collective-permute-start = (f32[16,40,128]{2,1,0:T(8,128)S(1)}, f32[16,40,128]{2,1,0:T(8,128)S(1)}, u32[]{:S(2)}, u32[]{:S(2)}) collective-permute-start(f32[16,40,128]{2,1,0:T(8,128)S(1)} %get-tuple-element.106), channel_id=1, source_target_pairs={{0,8},{8,16},{16,24},{1,9},{9,17},{17,25},{2,10},{10,18},{18,26},{... | collective-permute-start | bytes 983048 | tf_op jit(solution)/shard_map/ppermute | solution.py:608
  6.8 0.0 collective-permute-done.1.after_ref
  6.8 1.2 %collective-permute-done.before_ref = f32[16,40,128]{2,1,0:T(8,128)S(1)} collective-permute-done((f32[16,40,128]{2,1,0:T(8,128)S(1)}, f32[16,40,128]{2,1,0:T(8,128)S(1)}, u32[]{:S(2)}, u32[]{:S(2)}) %collective-permute-start) | collective-permute-done | bytes 327712 | tf_op jit(solution)/shard_map/ppermute | solution.py:608
  8.0 0.8 pack.1
  8.8 4.9 %collective-permute-start.2 = (f32[10,40,128]{2,1,0:T(8,128)S(1)}, f32[10,40,128]{2,1,0:T(8,128)S(1)}, u32[]{:S(2)}, u32[]{:S(2)}) collective-permute-start(f32[10,40,128]{2,1,0:T(8,128)S(1)} %get-tuple-element.55), channel_id=1, source_target_pairs={{0,1},{1,2},{2,3},{3,4},{4,5},{5,6},{6,7},{8,9},{9,10},{10,11},{11... | collective-permute-start | bytes 614408 | tf_op jit(solution)/shard_map/ppermute | solution.py:614
  13.8 1.3 %collective-permute-start.3 = (f32[10,40,128]{2,1,0:T(8,128)S(1)}, f32[10,40,128]{2,1,0:T(8,128)S(1)}, u32[]{:S(2)}, u32[]{:S(2)}) collective-permute-start(f32[10,40,128]{2,1,0:T(8,128)S(1)} %get-tuple-element.57), channel_id=1, source_target_pairs={{1,0},{2,1},{3,2},{4,3},{5,4},{6,5},{7,6},{9,8},{10,9},{11,10},{12... | collective-permute-start | bytes 614408 | tf_op jit(solution)/shard_map/ppermute | solution.py:615
  15.1 0.0 copy-done
  15.1 0.1 copy.10.raw_ref
  15.2 2.3 %krylov.1.refs_1_ = f32[160,128]{1,0:T(8,128)S(1)} custom-call(f32[4,37,34]{2,1,0:T(8,128)S(1)} %copy.10.raw_ref), custom_call_target="tpu_custom_call" | custom-call | tf_op jit(solution)/shard_map/krylov/pallas_call | solution.py:616
  17.5 0.0 collective-permute-done.2.left_ref
  17.5 3.9 %collective-permute-done.3.right_ref = f32[10,40,128]{2,1,0:T(8,128)S(1)} collective-permute-done((f32[10,40,128]{2,1,0:T(8,128)S(1)}, f32[10,40,128]{2,1,0:T(8,128)S(1)}, u32[]{:S(2)}, u32[]{:S(2)}) %collective-permute-start.3) | collective-permute-done | bytes 204832 | tf_op jit(solution)/shard_map/ppermute | solution.py:615
  21.4 6.9 %images.1 = (f32[80,40,128]{2,1,0:T(8,128)S(1)}, f32[80,40,128]{2,1,0:T(8,128)S(1)}, f32[8,80,128]{2,1,0:T(8,128)S(1)}, bf16[480,6144]{1,0:T(8,128)(2,1)S(1)}, f32[32,1,1024]{2,1,0:T(1,128)S(1)}) custom-call(f32[16,40,128]{2,1,0:T(8,128)S(1)} %collective-permute-done.before_ref, f32[48,40,128]{2,1,0:T(8,128)S(1)} %maximum_maximum_fusion.fields_ref, ...), custom_call_target="tpu_custom_call" | custom-call | tf_op jit(solution)/shard_map/images/pallas_call | solution.py:621
  28.3 18.1 %all_to_all.25.parts_ref = f32[32,1,1024]{2,1,0:T(1,128)S(1)} all-to-all(f32[32,1,1024]{2,1,0:T(1,128)S(1)} %get-tuple-element.58), channel_id=1, replica_groups=mesh['row'=4,'col'=8] {'row','col'}, dimensions={0} | all-to-all | bytes 262144 | tf_op jit(solution)/shard_map/all_to_all | solution.py:38
  46.4 0.1 relay.1
  46.5 10.0 %all_to_all.26.refs_0_ = f32[32,1,1024]{2,1,0:T(1,128)S(1)} all-to-all(f32[32,1,1024]{2,1,0:T(1,128)S(1)} %relay.1), channel_id=1, replica_groups=mesh['row'=4,'col'=8] {'row','col'}, dimensions={0} | all-to-all | bytes 262144 | tf_op jit(solution)/shard_map/all_to_all | solution.py:38
  56.5 6.7 %turn0.1 = (f32[32,1,1280]{2,1,0:T(1,128)S(1)}, f32[2,80,128]{2,1,0:T(8,128)S(1)}, bf16[16,6144]{1,0:T(8,128)(2,1)S(1)}, f32[48,128]{1,0:T(8,128)S(1)}, f32[40,2...) custom-call(f32[32,1,1024]{2,1,0:T(1,128)S(1)} %all_to_all.26.refs_0, ...), custom_call_target="tpu_custom_call" | custom-call | tf_op jit(solution)/shard_map/turn0/pallas_call | solution.py:662
  63.1 10.2 %all_to_all.27.refs_0_ = f32[32,1,1280]{2,1,0:T(1,128)S(1)} all-to-all(f32[32,1,1280]{2,1,0:T(1,128)S(1)} %get-tuple-element.64), channel_id=1, replica_groups=mesh['row'=4,'col'=8] {'row','col'}, dimensions={0} | all-to-all | bytes 327680 | tf_op jit(solution)/shard_map/all_to_all | solution.py:38
  73.3 5.7 %turn1.1 = (f32[32,1,1280]{2,1,0:T(1,128)S(1)}, f32[2,80,128]{2,1,0:T(8,128)S(1)}, bf16[16,6144]{1,0:T(8,128)(2,1)S(1)}, f32[48,128]{1,0:T(8,128)S(1)}, f32[40,2...) custom-call(f32[32,1,1280]{2,1,0:T(1,128)S(1)} %all_to_all.27.refs_0, ...), custom_call_target="tpu_custom_call" | custom-call | tf_op jit(solution)/shard_map/turn1/pallas_call | solution.py:662
  79.0 10.7 %all_to_all.28.refs_0_ = f32[32,1,1280]{2,1,0:T(1,128)S(1)} all-to-all(f32[32,1,1280]{2,1,0:T(1,128)S(1)} %get-tuple-element.73), channel_id=1, replica_groups=mesh['row'=4,'col'=8] {'row','col'}, dimensions={0} | all-to-all | bytes 327680 | tf_op jit(solution)/shard_map/all_to_all | solution.py:38
  89.7 5.8 %turn2.1 = (f32[32,1,1280]{2,1,0:T(1,128)S(1)}, f32[2,80,128]{2,1,0:T(8,128)S(1)}, bf16[16,6144]{1,0:T(8,128)(2,1)}, f32[48,128]{1,0:T(8,128)S(1)}, f32[40,256]{...) custom-call(f32[32,1,1280]{2,1,0:T(1,128)S(1)} %all_to_all.28.refs_0, ...), custom_call_target="tpu_custom_call" | custom-call | tf_op jit(solution)/shard_map/turn2/pallas_call | solution.py:662
  95.5 10.7 %all_to_all.29.refs_0_ = f32[32,1,1280]{2,1,0:T(1,128)S(1)} all-to-all(f32[32,1,1280]{2,1,0:T(1,128)S(1)} %get-tuple-element.82), channel_id=1, replica_groups=mesh['row'=4,'col'=8] {'row','col'}, dimensions={0} | all-to-all | bytes 327680 | tf_op jit(solution)/shard_map/all_to_all | solution.py:38
  106.2 3.7 %final.1 = (f32[3,48,128]{2,1,0:T(8,128)}, f32[37,4,40]{2,1,0:T(4,128)}, f32[3,37]{1,0:T(4,128)}, f32[5,5,40,40]{3,2,1,0:T(8,128)}, f32[3,48,128]{2,1,0:T(8,128)}) custom-call(f32[32,1,1280]{2,1,0:T(1,128)S(1)} %all_to_all.29.refs_0_, f32[40,256]{1,0:T(8,128)S(1)} %get-tuple-element.83.refs_1_, f32[40,128]{1,0:T(8,128)S(1)} %get-tuple-element.84.refs_2_, ...), custom_call_target="tpu_custom_call" | custom-call | tf_op jit(solution)/shard_map/final/pallas_call | solution.py:684
  (1 shorter events, 0.0 us)
Async XLA Ops:
  0.6 1.6 %copy-start.1 = (f32[48,128]{1,0:T(8,128)S(1)}, f32[48,128]{1,0:T(8,128)}, u32[]{:S(2)}) copy-start(f32[48,128]{1,0:T(8,128)} %param.7) | copy-start | bytes 73732
  0.6 1.6 %copy-start.2 = (f32[48,128]{1,0:T(8,128)S(1)}, f32[48,128]{1,0:T(8,128)}, u32[]{:S(2)}) copy-start(f32[48,128]{1,0:T(8,128)} %param.6) | copy-start | bytes 73732
  2.4 12.7 %copy-start = (f32[4,37,34]{1,0,2:T(4,128)S(1)}, f32[4,37,34]{1,0,2:T(4,128)}, u32[]{:S(2)}) copy-start(f32[4,37,34]{1,0,2:T(4,128)} %param.5) | copy-start | bytes 60388
  2.4 4.4 %collective-permute-start.1 = (f32[16,40,128]{2,1,0:T(8,128)S(1)}, f32[16,40,128]{2,1,0:T(8,128)S(1)}, u32[]{:S(2)}, u32[]{:S(2)}) collective-permute-start(f32[16,40,128]{2,1,0:T(8,128)S(1)} %get-tuple-element.105), channel_id=1, source_target_pairs={{8,0},{16,8},{24,16},{9,1},{17,9},{25,17},{10,2},{18,10},{26,18},{... | collective-permute-start | bytes 983048 | tf_op jit(solution)/shard_map/ppermute | solution.py:609
  3.7 4.3 %collective-permute-start = (f32[16,40,128]{2,1,0:T(8,128)S(1)}, f32[16,40,128]{2,1,0:T(8,128)S(1)}, u32[]{:S(2)}, u32[]{:S(2)}) collective-permute-start(f32[16,40,128]{2,1,0:T(8,128)S(1)} %get-tuple-element.106), channel_id=1, source_target_pairs={{0,8},{8,16},{16,24},{1,9},{9,17},{17,25},{2,10},{10,18},{18,26},{... | collective-permute-start | bytes 983048 | tf_op jit(solution)/shard_map/ppermute | solution.py:608
  8.8 8.7 %collective-permute-start.2 = (f32[10,40,128]{2,1,0:T(8,128)S(1)}, f32[10,40,128]{2,1,0:T(8,128)S(1)}, u32[]{:S(2)}, u32[]{:S(2)}) collective-permute-start(f32[10,40,128]{2,1,0:T(8,128)S(1)} %get-tuple-element.55), channel_id=1, source_target_pairs={{0,1},{1,2},{2,3},{3,4},{4,5},{5,6},{6,7},{8,9},{9,10},{10,11},{11... | collective-permute-start | bytes 614408 | tf_op jit(solution)/shard_map/ppermute | solution.py:614
  13.8 7.7 %collective-permute-start.3 = (f32[10,40,128]{2,1,0:T(8,128)S(1)}, f32[10,40,128]{2,1,0:T(8,128)S(1)}, u32[]{:S(2)}, u32[]{:S(2)}) collective-permute-start(f32[10,40,128]{2,1,0:T(8,128)S(1)} %get-tuple-element.57), channel_id=1, source_target_pairs={{1,0},{2,1},{3,2},{4,3},{5,4},{6,5},{7,6},{9,8},{10,9},{11,10},{12... | collective-permute-start | bytes 614408 | tf_op jit(solution)/shard_map/ppermute | solution.py:615

commit v6 on v5

--- a/solution.py
+++ b/solution.py
@@ -258,6 +258,7 @@
     level(3, (m2, s2), (m1, s1), (m3, s3), True)
     level(4, (m3, s3), (m2, s2), None, False)
 
+    acc_ref[:, size:] = jnp.zeros((2 * size, WIDE - size), F32)
     chunk = rows * cols // 3
     for i in range(3):
         place = slice(i * chunk, (i + 1) * chunk)

time: 110 us -> 110 us (level)
  no operation moved by 1% of the time
where the time goes in v6:
time: 110 us
  blocking collectives  59.5 us (54%)
  Pallas kernels  32 us (29%)
  starting transfers between devices  10.5 us (10%)
  waiting for transfers between devices  5.09 us (5%)
  local copies, waits for them, and re-layouts  1.74 us (2%)
    all_to_all x5, blocking collectives, exchange(): return lax.all_to_all(spread, AXES, 0, 0, tiled=True)  59.5 us
    pallas_call x3, Pallas kernels, local(): pl.pallas_call(functools.partial(turn_body, turn, inverse_total, count),...  18.2 us
    pallas_call x1, Pallas kernels, local(): pl.pallas_call(image_body, out_shape=(shape(total, K, cols), shape(total,...  6.88 us
    ppermute x1, starting transfers between devices, local(): from_left = lax.ppermute(high, 'col', up)  4.91 us
    ppermute x1, waiting for transfers between devices, local(): from_right = lax.ppermute(low, 'col', down)  3.88 us
    pallas_call x1, Pallas kernels, local(): pl.pallas_call(functools.partial(final_body, inverse_total), out_shape=(s...  3.69 us
    ppermute x1, starting transfers between devices, local(): before = lax.ppermute(fields[rows - HALO:], 'row', up)  3.05 us
    pallas_call x1, Pallas kernels, local(): pl.pallas_call(krylov_body, out_shape=shape(4 * K, PAD), name='krylov', c...  2.32 us
  transfers between devices with their start and end apart: 4, of which 2 were waited for; matrix products, arithmetic and copies ran while one was open for 0% of the time, Pallas kernels for 2%

profile of v6, /device:TPU:0, one launch (start us, length us, event | category | flops | bytes accessed | tf_op | source)
XLA Modules:
  0.0 109.9 jit_solution(163334047651737774)
XLA Ops:
  0.6 0.0 copy-start.1
  0.6 0.0 copy-start.2
  0.7 1.5 %copy.12 = f32[37,48,128]{2,0,1:T(8,128)S(1)} copy(f32[37,48,128]{2,1,0:T(8,128)} %param.4) | data formatting | bytes 1818624 | tf_op args[0]
  2.1 0.1 pad.3.clone
  2.2 0.0 copy-done.1
  2.2 0.0 copy-done.2
  2.2 0.1 maximum_maximum_fusion.fields_ref
  2.4 0.0 copy-start
  2.4 1.3 %collective-permute-start.1 = (f32[16,40,128]{2,1,0:T(8,128)S(1)}, f32[16,40,128]{2,1,0:T(8,128)S(1)}, u32[]{:S(2)}, u32[]{:S(2)}) collective-permute-start(f32[16,40,128]{2,1,0:T(8,128)S(1)} %get-tuple-element.105), channel_id=1, source_target_pairs={{8,0},{16,8},{24,16},{9,1},{17,9},{25,17},{10,2},{18,10},{26,18},{... | collective-permute-start | bytes 983048 | tf_op jit(solution)/shard_map/ppermute | solution.py:610
  3.7 3.1 %collective-permute-start = (f32[16,40,128]{2,1,0:T(8,128)S(1)}, f32[16,40,128]{2,1,0:T(8,128)S(1)}, u32[]{:S(2)}, u32[]{:S(2)}) collective-permute-start(f32[16,40,128]{2,1,0:T(8,128)S(1)} %get-tuple-element.106), channel_id=1, source_target_pairs={{0,8},{8,16},{16,24},{1,9},{9,17},{17,25},{2,10},{10,18},{18,26},{... | collective-permute-start | bytes 983048 | tf_op jit(solution)/shard_map/ppermute | solution.py:609
  6.8 0.0 collective-permute-done.1.after_ref
  6.8 1.2 %collective-permute-done.before_ref = f32[16,40,128]{2,1,0:T(8,128)S(1)} collective-permute-done((f32[16,40,128]{2,1,0:T(8,128)S(1)}, f32[16,40,128]{2,1,0:T(8,128)S(1)}, u32[]{:S(2)}, u32[]{:S(2)}) %collective-permute-start) | collective-permute-done | bytes 327712 | tf_op jit(solution)/shard_map/ppermute | solution.py:609
  8.0 0.8 pack.1
  8.8 4.9 %collective-permute-start.2 = (f32[10,40,128]{2,1,0:T(8,128)S(1)}, f32[10,40,128]{2,1,0:T(8,128)S(1)}, u32[]{:S(2)}, u32[]{:S(2)}) collective-permute-start(f32[10,40,128]{2,1,0:T(8,128)S(1)} %get-tuple-element.55), channel_id=1, source_target_pairs={{0,1},{1,2},{2,3},{3,4},{4,5},{5,6},{6,7},{8,9},{9,10},{10,11},{11... | collective-permute-start | bytes 614408 | tf_op jit(solution)/shard_map/ppermute | solution.py:615
  13.8 1.3 %collective-permute-start.3 = (f32[10,40,128]{2,1,0:T(8,128)S(1)}, f32[10,40,128]{2,1,0:T(8,128)S(1)}, u32[]{:S(2)}, u32[]{:S(2)}) collective-permute-start(f32[10,40,128]{2,1,0:T(8,128)S(1)} %get-tuple-element.57), channel_id=1, source_target_pairs={{1,0},{2,1},{3,2},{4,3},{5,4},{6,5},{7,6},{9,8},{10,9},{11,10},{12... | collective-permute-start | bytes 614408 | tf_op jit(solution)/shard_map/ppermute | solution.py:616
  15.1 0.0 copy-done
  15.1 0.1 copy.10.raw_ref
  15.2 2.3 %krylov.1.refs_1_ = f32[160,128]{1,0:T(8,128)S(1)} custom-call(f32[4,37,34]{2,1,0:T(8,128)S(1)} %copy.10.raw_ref), custom_call_target="tpu_custom_call" | custom-call | tf_op jit(solution)/shard_map/krylov/pallas_call | solution.py:617
  17.5 0.0 collective-permute-done.2.left_ref
  17.5 3.9 %collective-permute-done.3.right_ref = f32[10,40,128]{2,1,0:T(8,128)S(1)} collective-permute-done((f32[10,40,128]{2,1,0:T(8,128)S(1)}, f32[10,40,128]{2,1,0:T(8,128)S(1)}, u32[]{:S(2)}, u32[]{:S(2)}) %collective-permute-start.3) | collective-permute-done | bytes 204832 | tf_op jit(solution)/shard_map/ppermute | solution.py:616
  21.4 6.9 %images.1 = (f32[80,40,128]{2,1,0:T(8,128)S(1)}, f32[80,40,128]{2,1,0:T(8,128)S(1)}, f32[8,80,128]{2,1,0:T(8,128)S(1)}, bf16[480,6144]{1,0:T(8,128)(2,1)S(1)}, f32[32,1,1024]{2,1,0:T(1,128)S(1)}) custom-call(f32[16,40,128]{2,1,0:T(8,128)S(1)} %collective-permute-done.before_ref, f32[48,40,128]{2,1,0:T(8,128)S(1)} %maximum_maximum_fusion.fields_ref, ...), custom_call_target="tpu_custom_call" | custom-call | tf_op jit(solution)/shard_map/images/pallas_call | solution.py:622
  28.3 18.1 %all_to_all.25.parts_ref = f32[32,1,1024]{2,1,0:T(1,128)S(1)} all-to-all(f32[32,1,1024]{2,1,0:T(1,128)S(1)} %get-tuple-element.58), channel_id=1, replica_groups=mesh['row'=4,'col'=8] {'row','col'}, dimensions={0} | all-to-all | bytes 262144 | tf_op jit(solution)/shard_map/all_to_all | solution.py:38
  46.4 0.1 relay.1
  46.5 10.0 %all_to_all.26.refs_0_ = f32[32,1,1024]{2,1,0:T(1,128)S(1)} all-to-all(f32[32,1,1024]{2,1,0:T(1,128)S(1)} %relay.1), channel_id=1, replica_groups=mesh['row'=4,'col'=8] {'row','col'}, dimensions={0} | all-to-all | bytes 262144 | tf_op jit(solution)/shard_map/all_to_all | solution.py:38
  56.5 6.7 %turn0.1 = (f32[32,1,1280]{2,1,0:T(1,128)S(1)}, f32[2,80,128]{2,1,0:T(8,128)S(1)}, bf16[16,6144]{1,0:T(8,128)(2,1)S(1)}, f32[48,128]{1,0:T(8,128)S(1)}, f32[40,2...) custom-call(f32[32,1,1024]{2,1,0:T(1,128)S(1)} %all_to_all.26.refs_0, ...), custom_call_target="tpu_custom_call" | custom-call | tf_op jit(solution)/shard_map/turn0/pallas_call | solution.py:663
  63.1 10.2 %all_to_all.27.refs_0_ = f32[32,1,1280]{2,1,0:T(1,128)S(1)} all-to-all(f32[32,1,1280]{2,1,0:T(1,128)S(1)} %get-tuple-element.64), channel_id=1, replica_groups=mesh['row'=4,'col'=8] {'row','col'}, dimensions={0} | all-to-all | bytes 327680 | tf_op jit(solution)/shard_map/all_to_all | solution.py:38
  73.3 5.7 %turn1.1 = (f32[32,1,1280]{2,1,0:T(1,128)S(1)}, f32[2,80,128]{2,1,0:T(8,128)S(1)}, bf16[16,6144]{1,0:T(8,128)(2,1)S(1)}, f32[48,128]{1,0:T(8,128)S(1)}, f32[40,2...) custom-call(f32[32,1,1280]{2,1,0:T(1,128)S(1)} %all_to_all.27.refs_0, ...), custom_call_target="tpu_custom_call" | custom-call | tf_op jit(solution)/shard_map/turn1/pallas_call | solution.py:663
  79.0 10.7 %all_to_all.28.refs_0_ = f32[32,1,1280]{2,1,0:T(1,128)S(1)} all-to-all(f32[32,1,1280]{2,1,0:T(1,128)S(1)} %get-tuple-element.73), channel_id=1, replica_groups=mesh['row'=4,'col'=8] {'row','col'}, dimensions={0} | all-to-all | bytes 327680 | tf_op jit(solution)/shard_map/all_to_all | solution.py:38
  89.7 5.8 %turn2.1 = (f32[32,1,1280]{2,1,0:T(1,128)S(1)}, f32[2,80,128]{2,1,0:T(8,128)S(1)}, bf16[16,6144]{1,0:T(8,128)(2,1)}, f32[48,128]{1,0:T(8,128)S(1)}, f32[40,256]{...) custom-call(f32[32,1,1280]{2,1,0:T(1,128)S(1)} %all_to_all.28.refs_0, ...), custom_call_target="tpu_custom_call" | custom-call | tf_op jit(solution)/shard_map/turn2/pallas_call | solution.py:663
  95.5 10.7 %all_to_all.29.refs_0_ = f32[32,1,1280]{2,1,0:T(1,128)S(1)} all-to-all(f32[32,1,1280]{2,1,0:T(1,128)S(1)} %get-tuple-element.82), channel_id=1, replica_groups=mesh['row'=4,'col'=8] {'row','col'}, dimensions={0} | all-to-all | bytes 327680 | tf_op jit(solution)/shard_map/all_to_all | solution.py:38
  106.2 3.7 %final.1 = (f32[3,48,128]{2,1,0:T(8,128)}, f32[37,4,40]{2,1,0:T(4,128)}, f32[3,37]{1,0:T(4,128)}, f32[5,5,40,40]{3,2,1,0:T(8,128)}, f32[3,48,128]{2,1,0:T(8,128)}) custom-call(f32[32,1,1280]{2,1,0:T(1,128)S(1)} %all_to_all.29.refs_0_, f32[40,256]{1,0:T(8,128)S(1)} %get-tuple-element.83.refs_1_, f32[40,128]{1,0:T(8,128)S(1)} %get-tuple-element.84.refs_2_, ...), custom_call_target="tpu_custom_call" | custom-call | tf_op jit(solution)/shard_map/final/pallas_call | solution.py:685
  (1 shorter events, 0.0 us)
Async XLA Ops:
  0.6 1.6 %copy-start.1 = (f32[48,128]{1,0:T(8,128)S(1)}, f32[48,128]{1,0:T(8,128)}, u32[]{:S(2)}) copy-start(f32[48,128]{1,0:T(8,128)} %param.7) | copy-start | bytes 73732
  0.6 1.6 %copy-start.2 = (f32[48,128]{1,0:T(8,128)S(1)}, f32[48,128]{1,0:T(8,128)}, u32[]{:S(2)}) copy-start(f32[48,128]{1,0:T(8,128)} %param.6) | copy-start | bytes 73732
  2.4 12.7 %copy-start = (f32[4,37,34]{1,0,2:T(4,128)S(1)}, f32[4,37,34]{1,0,2:T(4,128)}, u32[]{:S(2)}) copy-start(f32[4,37,34]{1,0,2:T(4,128)} %param.5) | copy-start | bytes 60388
  2.4 4.4 %collective-permute-start.1 = (f32[16,40,128]{2,1,0:T(8,128)S(1)}, f32[16,40,128]{2,1,0:T(8,128)S(1)}, u32[]{:S(2)}, u32[]{:S(2)}) collective-permute-start(f32[16,40,128]{2,1,0:T(8,128)S(1)} %get-tuple-element.105), channel_id=1, source_target_pairs={{8,0},{16,8},{24,16},{9,1},{17,9},{25,17},{10,2},{18,10},{26,18},{... | collective-permute-start | bytes 983048 | tf_op jit(solution)/shard_map/ppermute | solution.py:610
  3.7 4.3 %collective-permute-start = (f32[16,40,128]{2,1,0:T(8,128)S(1)}, f32[16,40,128]{2,1,0:T(8,128)S(1)}, u32[]{:S(2)}, u32[]{:S(2)}) collective-permute-start(f32[16,40,128]{2,1,0:T(8,128)S(1)} %get-tuple-element.106), channel_id=1, source_target_pairs={{0,8},{8,16},{16,24},{1,9},{9,17},{17,25},{2,10},{10,18},{18,26},{... | collective-permute-start | bytes 983048 | tf_op jit(solution)/shard_map/ppermute | solution.py:609
  8.8 8.7 %collective-permute-start.2 = (f32[10,40,128]{2,1,0:T(8,128)S(1)}, f32[10,40,128]{2,1,0:T(8,128)S(1)}, u32[]{:S(2)}, u32[]{:S(2)}) collective-permute-start(f32[10,40,128]{2,1,0:T(8,128)S(1)} %get-tuple-element.55), channel_id=1, source_target_pairs={{0,1},{1,2},{2,3},{3,4},{4,5},{5,6},{6,7},{8,9},{9,10},{10,11},{11... | collective-permute-start | bytes 614408 | tf_op jit(solution)/shard_map/ppermute | solution.py:615
  13.8 7.7 %collective-permute-start.3 = (f32[10,40,128]{2,1,0:T(8,128)S(1)}, f32[10,40,128]{2,1,0:T(8,128)S(1)}, u32[]{:S(2)}, u32[]{:S(2)}) collective-permute-start(f32[10,40,128]{2,1,0:T(8,128)S(1)} %get-tuple-element.57), channel_id=1, source_target_pairs={{1,0},{2,1},{3,2},{4,3},{5,4},{6,5},{7,6},{9,8},{10,9},{11,10},{12... | collective-permute-start | bytes 614408 | tf_op jit(solution)/shard_map/ppermute | solution.py:616
